TPU v7x, 256 devices: a whole 4x4x8 slice. The times are simulated.
256 devices in a mesh: dp: 16 (over y, x_hi, core), proto: 16 (over x_lo, z).
Axes of the slice: x: 4 (x_hi: 2, x_lo: 2; x = x_hi * 2 + x_lo), y: 4, z: 8, core: 2. Of those that a mesh axis runs over, the one named last changes fastest.
Arguments:
- hidden_states: bfloat16 [512, 256, 2048], P(('dp', 'proto')), may hold values from -15 to 30, as said below
- teacher_feats: bfloat16 [512, 256, 384], P(('dp', 'proto')), may hold values from -25 to 25, as said below
- masks: int32 [512, 32], P(('dp', 'proto')), may hold values from 0 to 255, as said below
- head_weight: bfloat16 [2048, 384], replicated, as said below
- prototypes: bfloat16 [49152, 384], P('proto'), may hold values from -25 to 25, as said below
- center: float32 [49152], P('proto'), may hold values from -1.8 to 1.8
Outputs:
- loss: float32 [], replicated
- grad_hidden: bfloat16 [16384, 2048], P(('dp', 'proto'))
- grad_head: float32 [2048, 384], P(('dp', 'proto'))
Inputs may be any that keep to these rules, and one draw needn't show every extreme that they name: `masks`: each row lists 32 different patch numbers of its image. `hidden_states`: independent entries. `teacher_feats`: independent entries. `head_weight`: independent entries of deviation 2048 ** -0.5. `prototypes`: independent entries.
All inputs are finite; a program needn't handle non-finite values.
Results may differ from a plain program's by a relative error of at most 0.00305.
The roundings to bfloat16 on the way count: a program that leaves them out, or rounds other values in their place, can miss the bound.
Values may be sent and summed in bfloat16 or wider, within the bound.
A program may use at most 64 MiB of HBM per device.

v0:
```python
import math

import jax
import jax.numpy as jnp
from jax import lax
from jax.sharding import Mesh
from jax.sharding import PartitionSpec as P

PROTO = ("proto_0", "proto_1")
DP_PROTO = ("dp", "proto_0", "proto_1")


STUDENT_TEMP = 0.1
TEACHER_TEMP = 0.07
LOSS_SCALE = 524288.0
EPSILON = 1e-06


def in_order(blocks, dim):
    blocks = jnp.moveaxis(blocks, 0, dim)
    shape = blocks.shape
    return blocks.reshape(*shape[:dim], shape[dim] * shape[dim + 1], *shape[dim + 2 :])


def stacked_from(array, axes, sequence):
    blocks = array
    for k in sequence:
        blocks = lax.all_gather(blocks, axes[k])
    done = sequence[::-1]
    back = [done.index(k) for k in range(len(axes))]
    blocks = blocks.transpose(*back, *range(len(axes), blocks.ndim))
    return blocks.reshape(-1, *array.shape)


def whole_of(array, axes, sequence, dim):
    return in_order(stacked_from(array, axes, sequence), dim)


def sent_to_all(array, axis):
    peers = lax.axis_size(axis)
    return lax.all_to_all(
        jnp.broadcast_to(array[None], (peers, *array.shape)), axis, 0, 0, tiled=True
    )


def all_in_one(array, axis):
    leaves = jax.tree.leaves(array)
    sequence = sorted(range(len(leaves)), key=lambda k: -leaves[k].size)
    width = (1, *leaves[sequence[0]].shape)[-1]
    lines = [
        jnp.pad(leaves[k].reshape(-1), (0, -leaves[k].size % width)).reshape(-1, width)
        for k in sequence
    ]
    both, at, found = (sent_to_all(jnp.concatenate(lines), axis), 0, {})
    for k, line in zip(sequence, lines):
        piece = both[:, at : at + len(line)].reshape(len(both), -1)
        found[k] = piece[:, : leaves[k].size].reshape(-1, *leaves[k].shape)
        at += len(line)
    numbers = iter(range(len(leaves)))
    return jax.tree.map(lambda _: found[next(numbers)], array)


def joined_by_halves(pieces, combine):
    while len(jax.tree.leaves(pieces)[0]) > 1:
        pieces = jax.vmap(combine)(
            *(jax.tree.map(lambda part: part[side::2], pieces) for side in (0, 1))
        )
    return jax.tree.map(lambda part: part[0], pieces)


def combined_all(array, axis, combine):
    pieces = all_in_one(array, axis)
    return joined_by_halves(pieces, combine)


def of_everyone(array, axis):
    return sent_to_all(array, axis).sum(axis=0)


def in_blocks(array, dim, peers):
    shape = array.shape
    blocks = array.reshape(*shape[:dim], peers, shape[dim] // peers, *shape[dim + 1 :])
    return jnp.moveaxis(blocks, dim, 0)


def summed_on_arrival(array, axis, dim):
    peers = lax.axis_size(axis)
    blocks = lax.all_to_all(in_blocks(array, dim, peers), axis, 0, 0, tiled=True)
    return jnp.sum(blocks, axis=0)


def unit_rows(feats):
    radius = jnp.sqrt(jnp.sum(feats * feats, axis=-1, keepdims=True) + EPSILON)
    return (feats / radius, radius)


def block_logits(student, teacher, protos, center, first, width):
    tile = lax.dynamic_slice_in_dim(protos, first, width, 0)
    offset = lax.dynamic_slice_in_dim(center, first, width, 0)
    dims = (((1,), (1,)), ((), ()))
    s_logits = (
        lax.dot_general(student, tile, dims, preferred_element_type=jnp.float32) / STUDENT_TEMP
    )
    t_logits = (
        lax.dot_general(teacher, tile, dims, preferred_element_type=jnp.float32) - offset[None, :]
    ) / TEACHER_TEMP
    return (s_logits, t_logits, tile)


def row_stats(student, teacher, protos, center):
    count = student.shape[0]
    width = math.gcd(protos.shape[0], 1536)

    def row_step(index, state):
        peak_s, total_s, peak_t, total_t, cross = state
        s_logits, t_logits, tile = block_logits(
            student, teacher, protos, center, index * width, width
        )
        new_s = jnp.maximum(peak_s, jnp.max(s_logits, axis=1))
        total_s = total_s * jnp.exp(peak_s - new_s) + jnp.sum(
            jnp.exp(s_logits - new_s[:, None]), axis=1
        )
        new_t = jnp.maximum(peak_t, jnp.max(t_logits, axis=1))
        weights = jnp.exp(t_logits - new_t[:, None])
        rescale = jnp.exp(peak_t - new_t)
        total_t = total_t * rescale + jnp.sum(weights, axis=1)
        cross = cross * rescale + jnp.sum(weights * s_logits, axis=1)
        return (new_s, total_s, new_t, total_t, cross)

    lowest = jnp.full((count,), -jnp.inf, jnp.float32)
    zeros = jnp.zeros((count,), jnp.float32)
    return lax.fori_loop(
        0, protos.shape[0] // width, row_step, (lowest, zeros, lowest, zeros, zeros)
    )


def join_stats(first, second):
    peak_s = jnp.maximum(first[0], second[0])
    peak_t = jnp.maximum(first[2], second[2])
    left_s = jnp.exp(first[0] - peak_s)
    right_s = jnp.exp(second[0] - peak_s)
    left_t = jnp.exp(first[2] - peak_t)
    right_t = jnp.exp(second[2] - peak_t)
    total_s = first[1] * left_s + second[1] * right_s
    total_t = first[3] * left_t + second[3] * right_t
    cross = first[4] * left_t + second[4] * right_t
    return (peak_s, total_s, peak_t, total_t, cross)


def per_device(hidden_states, teacher_feats, masks, head_weight, prototypes, center):
    local_rows = masks.shape[0] * masks.shape[1]
    picked = jnp.take_along_axis(hidden_states, masks[:, :, None], axis=1).reshape(
        local_rows, hidden_states.shape[2]
    )
    teacher_rows = jnp.take_along_axis(teacher_feats, masks[:, :, None], axis=1).reshape(
        local_rows, teacher_feats.shape[2]
    )
    raw = jnp.dot(picked, head_weight, preferred_element_type=jnp.float32)
    unit, radius = unit_rows(raw)
    student = unit.astype(jnp.bfloat16)
    teacher = unit_rows(teacher_rows.astype(jnp.float32))[0].astype(jnp.bfloat16)
    bottleneck = head_weight.shape[1]
    group = lax.axis_size(PROTO)
    group_rows = local_rows * group
    total_rows = group_rows * lax.axis_size("dp")
    factor = LOSS_SCALE / (total_rows * STUDENT_TEMP)
    width = math.gcd(prototypes.shape[0], 1536)
    blocks = prototypes.shape[0] // width
    piece = (whole_of(student, PROTO, (0, 1), 0), whole_of(teacher, PROTO, (0, 1), 0))
    found = row_stats(piece[0], piece[1], prototypes, center)
    collect_stu_all = piece[0]
    collect_tea_all = piece[1]
    collect_peak_s = found[0]
    collect_total_s = found[1]
    collect_peak_t = found[2]
    collect_total_t = found[3]
    cross = found[4]
    stu_all, tea_all, peak_s, total_s, peak_t, total_t, cross = (
        collect_stu_all,
        collect_tea_all,
        collect_peak_s,
        collect_total_s,
        collect_peak_t,
        collect_total_t,
        cross,
    )
    peak_s, total_s, peak_t, total_t, cross = combined_all(
        (peak_s, total_s, peak_t, total_t, cross), PROTO, join_stats
    )
    row_loss = peak_s + jnp.log(total_s) - cross / total_t
    loss = of_everyone(jnp.sum(row_loss), "dp") / total_rows
    top_s = peak_s[:, None]
    sum_s = total_s[:, None]
    top_t = peak_t[:, None]
    sum_t = total_t[:, None]

    def gradient_step(index, acc):
        s_logits, t_logits, tile = block_logits(
            stu_all, tea_all, prototypes, center, index * width, width
        )
        prob = jnp.exp(s_logits - top_s) / sum_s
        target = jnp.exp(t_logits - top_t) / sum_t
        grads = (factor * (prob - target)).astype(jnp.bfloat16)
        return acc + jnp.dot(grads, tile, preferred_element_type=jnp.float32)

    back = summed_on_arrival(
        lax.fori_loop(
            0,
            blocks,
            gradient_step,
            jnp.zeros((local_rows * lax.axis_size(PROTO), bottleneck), jnp.float32),
        ),
        PROTO,
        0,
    )
    inner = jnp.sum(unit * back, axis=-1, keepdims=True)
    direction = ((back - unit * inner) / radius).astype(jnp.bfloat16)
    grad_hidden = lax.dot_general(
        direction, head_weight, (((1,), (1,)), ((), ())), preferred_element_type=jnp.float32
    ).astype(jnp.bfloat16)
    share = head_weight.shape[0] // (lax.axis_size("dp") * lax.axis_size(PROTO))
    full = jnp.dot(picked.T, direction, preferred_element_type=jnp.float32)
    summed = lax.psum(full, DP_PROTO)
    position = lax.axis_index("dp") * lax.axis_size(PROTO) + lax.axis_index(PROTO)
    grad_head = lax.dynamic_slice_in_dim(summed, position * share, share, 0)
    return (loss, grad_hidden, grad_head)


def solution(mesh):
    finer = Mesh(mesh.devices.reshape(mesh.shape["dp"], 2, 8), ("dp", "proto_0", "proto_1"))
    placed = (
        P(DP_PROTO, None, None),
        P(DP_PROTO, None, None),
        P(DP_PROTO, None),
        P(),
        P(PROTO, None),
        P(PROTO),
    )
    return jax.shard_map(
        per_device,
        mesh=finer,
        in_specs=placed,
        out_specs=(P(), P(DP_PROTO, None), P(DP_PROTO, None)),
        check_vma=False,
    )
```

profile of v0, /device:TPU:1, one launch (start us, length us, event | category | flops | bytes accessed | tf_op | source)
XLA Modules:
  0.0 465.8 jit_solution(8488720203513850521)
XLA Ops:
  7.2 0.0 copy-start
  7.2 0.0 copy-start.6
  7.2 0.0 copy-start.5
  7.2 0.8 compare_and_fusion
  8.0 0.7 bitcast_or_fusion
  8.7 0.1 broadcast_in_dim.62
  8.8 0.1 reshape.168
  8.9 0.0 copy-done
  8.9 1.5 gather_fusion
  10.4 0.0 copy-start.3
  10.4 2.0 multiply_reduce_fusion.4
  12.5 0.1 fusion.30
  12.6 4.2 all-gather
  16.7 24.6 %all-gather.1 = bf16[16,64,384]{2,1,0:T(8,128)(2,1)S(1)} all-gather(bf16[2,64,384]{2,1,0:T(8,128)(2,1)S(1)} %bitcast.75), channel_id=3, replica_groups=mesh['dp'=16,'proto_0'=2,'proto_1'=8] {'proto_1'}, dimensions={0}, use_global_device_ids=true | all-gather | bytes 884736 | tf_op jit(solution)/shard_map/all_gather | solution.py:28
  41.4 0.0 copy-done.1
  41.4 0.1 copy.23
  41.5 0.0 copy-done.6
  41.5 0.9 gather_fusion.1
  42.4 0.2 multiply_reduce_fusion.3
  42.5 0.1 sqrt.21
  42.6 0.1 divide_convert_fusion.1
  42.7 3.9 all_gather.26
  46.6 20.4 %all-gather.2 = bf16[16,64,384]{2,1,0:T(8,128)(2,1)S(1)} all-gather(bf16[2,64,384]{2,1,0:T(8,128)(2,1)S(1)} %all_gather.26), channel_id=4, replica_groups=mesh['dp'=16,'proto_0'=2,'proto_1'=8] {'proto_1'}, dimensions={0}, use_global_device_ids=true | all-gather | bytes 884736 | tf_op jit(solution)/shard_map/all_gather | solution.py:28
  67.1 1.0 copy.24
  68.1 0.0 copy-done.9
  68.1 26.3 %while.36 = (s32[]{:T(128)}, f32[1024]{0:T(1024)S(1)}, f32[1024]{0:T(1024)S(1)}, f32[1024]{0:T(1024)S(1)}, f32[1024]{0:T(1024)S(1)}, /*index=5*/f32[1024]{0:T(10...) while((s32[]{:T(128)}, f32[1024]{0:T(1024)S(1)}, ...), condition=%wide.region_8.9_spmd.clone, body=%wide.region_2.8_spmd.clone.sunk | while | flops 2437951488 | bytes 48120056 | solution.py:132
  68.1 0.1 dynamic_slice.59
  68.2 6.0 %fusion.52 = (f32[1024]{0:T(1024)S(1)}, f32[1536,1024]{1,0:T(8,128)}) fusion(f32[1536]{0:T(1024)S(1)} %dynamic_slice.59, bf16[1024,384]{1,0:T(8,128)(2,1)} %get-tuple-element.673, bf16[3072,384]{1,0:T(8,128)(2,1)} %get-tuple-element.671, s32[]{:T(128)S(6)} %select_n.72), kind=kOutput, calls=%fused_computation.6.clone.1 | convolution fusion | flops 1212677120 | bytes 8267780 | tf_op jit(solution)/shard_map/while/body/eval_jaxpr/dot_general | solution.py:105
  74.2 3.3 multiply_reduce_fusion.7
  77.5 3.7 multiply_reduce_fusion.8
  81.3 0.1 dynamic_slice.59
  81.4 6.0 %fusion.52 = (f32[1024]{0:T(1024)S(1)}, f32[1536,1024]{1,0:T(8,128)}) fusion(f32[1536]{0:T(1024)S(1)} %dynamic_slice.59, bf16[1024,384]{1,0:T(8,128)(2,1)} %get-tuple-element.673, bf16[3072,384]{1,0:T(8,128)(2,1)} %get-tuple-element.671, s32[]{:T(128)S(6)} %select_n.72), kind=kOutput, calls=%fused_computation.6.clone.1 | convolution fusion | flops 1212677120 | bytes 8267780 | tf_op jit(solution)/shard_map/while/body/eval_jaxpr/dot_general | solution.py:105
  87.3 3.3 multiply_reduce_fusion.7
  90.6 0.0 slice-done
  90.6 0.0 slice-done.1
  90.7 3.7 multiply_reduce_fusion.8
  94.4 0.8 broadcast_in_dim.69
  95.3 5.6 %all-to-all-start = ((f32[16,5,1024]{2,1,0:T(8,128)}), f32[16,5,1024]{2,1,0:T(8,128)S(1)}, u32[]{:S(2)}, u32[]{:S(2)}) async-start(f32[16,5,1024]{2,1,0:T(8,128)} %broadcast_in_dim.69), calls=%async_computation | async-start | bytes 1048576 | tf_op jit(solution)/shard_map/all_to_all | solution.py:41
  100.9 0.2 all-reduce.2.cloned.1.call-start
  101.1 10.1 %all-to-all-done = f32[16,5,1024]{2,1,0:T(8,128)S(1)} async-done(((f32[16,5,1024]{2,1,0:T(8,128)}), f32[16,5,1024]{2,1,0:T(8,128)S(1)}, u32[]{:S(2)}, u32[]{:S(2)}) %all-to-all-start) | async-done | bytes 327712 | tf_op jit(solution)/shard_map/all_to_all | solution.py:41
  111.2 0.8 fusion.33
  112.4 0.9 copy_bitcast_fusion
  113.9 0.7 subtract_reduce_fusion
  114.6 31.9 %while.37 = (s32[]{:T(128)}, f32[1024,384]{1,0:T(8,128)}, bf16[3072,384]{1,0:T(8,128)(2,1)}, bf16[1024,384]{1,0:T(8,128)(2,1)S(1)}, f32[1024,1]{0,1:T(1,128)S(1)...) while((s32[]{:T(128)}, f32[1024,384]{1,0:T(8,128)}, ...), condition=%wide.region_12.13_spmd.clone, body=%wide.region_11.12_spmd.clone.sunk | while | flops 3640393728 | bytes 20876996 | solution.py:207
  114.6 5.8 %fusion.59 = f32[1536,1024]{1,0:T(8,128)} fusion(bf16[1024,384]{1,0:T(8,128)(2,1)S(1)} %get-tuple-element.710, bf16[3072,384]{1,0:T(8,128)(2,1)} %get-tuple-element.709, s32[]{:T(128)S(6)} %select_n.73), kind=kOutput, calls=%fused_computation.28.clone.1 | convolution fusion | flops 1207959552 | bytes 8257540 | tf_op jit(solution)/shard_map/while/body/eval_jaxpr/dot_general | solution.py:102
  120.4 0.1 dynamic_slice.63
  120.5 9.9 %select_add_fusion.2 = f32[1024,384]{1,0:T(8,128)} fusion(f32[1024,384]{1,0:T(8,128)} %get-tuple-element.694, f32[1536,1024]{1,0:T(8,128)} %fusion.59, bf16[1024,384]{1,0:T(8,128)(2,1)} %get-tuple-element.713, f32[1024]{0:T(1024)S(1)} %bitcast.82, f32[1024]{0:T(1024)S(1)} %bitcast.84, f32[1536]{0:T(1024)S(1)} %dynamic_slice.63, ...), kind=kOutput, calls=%fused_computation.25.clone.1 | convolution fusion | flops 2432434176 | bytes 12606976 | tf_op jit(solution)/shard_map/while/body/eval_jaxpr/dot_general | solution.py:204
  130.3 5.7 %fusion.59 = f32[1536,1024]{1,0:T(8,128)} fusion(bf16[1024,384]{1,0:T(8,128)(2,1)S(1)} %get-tuple-element.710, bf16[3072,384]{1,0:T(8,128)(2,1)} %get-tuple-element.709, s32[]{:T(128)S(6)} %select_n.73), kind=kOutput, calls=%fused_computation.28.clone.1 | convolution fusion | flops 1207959552 | bytes 8257540 | tf_op jit(solution)/shard_map/while/body/eval_jaxpr/dot_general | solution.py:102
  136.1 0.1 dynamic_slice.63
  136.2 10.3 %select_add_fusion.2 = f32[1024,384]{1,0:T(8,128)} fusion(f32[1024,384]{1,0:T(8,128)} %get-tuple-element.694, f32[1536,1024]{1,0:T(8,128)} %fusion.59, bf16[1024,384]{1,0:T(8,128)(2,1)} %get-tuple-element.713, f32[1024]{0:T(1024)S(1)} %bitcast.82, f32[1024]{0:T(1024)S(1)} %bitcast.84, f32[1536]{0:T(1024)S(1)} %dynamic_slice.63, ...), kind=kOutput, calls=%fused_computation.25.clone.1 | convolution fusion | flops 2432434176 | bytes 12606976 | tf_op jit(solution)/shard_map/while/body/eval_jaxpr/dot_general | solution.py:204
  146.5 26.0 %all_to_all.16 = f32[16,64,384]{2,1,0:T(8,128)} all-to-all(f32[16,64,384]{2,1,0:T(8,128)} %bitcast.70), channel_id=1, replica_groups=mesh['dp'=16,'proto_0'=2,'proto_1'=8] {'proto_0','proto_1'}, dimensions={0} | all-to-all | bytes 3145728 | tf_op jit(solution)/shard_map/all_to_all | solution.py:88
  172.5 1.5 reduce_sum.97
  174.0 0.0 copy-done.2
  174.0 0.0 copy-done.8
  174.0 0.2 multiply_reduce_fusion.2
  174.2 2.3 fusion.22
  176.5 0.0 all-reduce.2.cloned.1.call-update
  176.6 1.3 broadcast_in_dim.70
  177.8 24.2 %all-to-all-start.1 = ((f32[16,1,1]{2,1,0:T(1,128)}), f32[16,1,1]{2,1,0:T(1,128)S(1)}, u32[]{:S(2)}, u32[]{:S(2)}) async-start(f32[16,1,1]{2,1,0:T(1,128)} %broadcast_in_dim.70), calls=%async_computation.1 | async-start | bytes 16384 | tf_op jit(solution)/shard_map/all_to_all | solution.py:41
  202.0 6.9 %all-to-all-done.1 = f32[16,1,1]{2,1,0:T(1,128)S(1)} async-done(((f32[16,1,1]{2,1,0:T(1,128)}), f32[16,1,1]{2,1,0:T(1,128)S(1)}, u32[]{:S(2)}, u32[]{:S(2)}) %all-to-all-start.1) | async-done | bytes 96 | tf_op jit(solution)/shard_map/all_to_all | solution.py:41
  208.9 0.6 reduce_sum.96
  210.2 2.7 convolution_convert_fusion
  212.9 243.5 %all-reduce.2.cloned.1.call-done = f32[2048,384]{1,0:T(8,128)} async-done(((f32[2048,384]{1,0:T(8,128)}), f32[2048,384]{1,0:T(8,128)}) %all-reduce.2.cloned.1.call-update) | async-done | bytes 3145744 | tf_op jit(solution)/shard_map/psum | solution.py:223
  456.5 1.3 constant_dynamic-slice_fusion
  (80 shorter events, 1.1 us)
Async XLA Ops:
  7.2 1.8 copy-start
  7.2 34.3 %copy-start.6 = (bf16[2,256,384]{2,1,0:T(8,128)(2,1)S(1)}, bf16[2,256,384]{2,1,0:T(8,128)(2,1)}, u32[]{:S(2)}) copy-start(bf16[2,256,384]{2,1,0:T(8,128)(2,1)} %param.11) | copy-start | bytes 1179652
  7.2 60.9 %copy-start.5 = (f32[3072]{0:T(1024)S(1)}, f32[3072]{0:T(1024)}, u32[]{:S(2)}) copy-start(f32[3072]{0:T(1024)} %param.15) | copy-start | bytes 36868
  8.8 59.3 %copy-start.9 = (pred[64]{0:T(512)(128)(4,1)}, pred[64]{0:T(512)(128)(4,1)S(1)}, u32[]{:S(2)}) copy-start(pred[64]{0:T(512)(128)(4,1)S(1)} %broadcast_in_dim.62) | copy-start | bytes 196
  10.4 31.0 %copy-start.3 = (bf16[64,2048]{1,0:T(8,128)(2,1)}, bf16[64,2048]{1,0:T(8,128)(2,1)S(1)}, u32[]{:S(2)}) copy-start(bf16[64,2048]{1,0:T(8,128)(2,1)S(1)} %gather_fusion) | copy-start | bytes 786436
  12.5 28.9 %copy-start.1 = (f32[64,384]{1,0:T(8,128)}, f32[64,384]{1,0:T(8,128)S(1)}, u32[]{:S(2)}) copy-start(f32[64,384]{1,0:T(8,128)S(1)} %get-tuple-element.490) | copy-start | bytes 294916
  12.5 55.7 %copy-start.7 = (f32[64]{0:T(128)}, f32[64]{0:T(128)S(1)}, u32[]{:S(2)}) copy-start(f32[64]{0:T(128)S(1)} %add_sqrt_fusion.1) | copy-start | bytes 772
  74.2 3.3 slice-start
  74.2 3.3 slice-start.1
  87.3 3.3 slice-start
  87.3 3.3 slice-start.1
  95.3 15.9 %all-to-all-start = ((f32[16,5,1024]{2,1,0:T(8,128)}), f32[16,5,1024]{2,1,0:T(8,128)S(1)}, u32[]{:S(2)}, u32[]{:S(2)}) async-start(f32[16,5,1024]{2,1,0:T(8,128)} %broadcast_in_dim.69), calls=%async_computation | async-start | bytes 1048576 | tf_op jit(solution)/shard_map/all_to_all | solution.py:41
  100.9 355.6 %all-reduce.2.cloned.1.call-start = ((), (), s32[]{:S(2)}) async-start(), calls=%async_computation.3 | async-start | bytes 6291456 | tf_op jit(solution)/shard_map/psum | solution.py:223
  114.6 59.4 %copy-start.2 = (f32[64,384]{1,0:T(8,128)S(1)}, f32[64,384]{1,0:T(8,128)}, u32[]{:S(2)}) copy-start(f32[64,384]{1,0:T(8,128)} %copy-done.1) | copy-start | bytes 294916
  114.6 59.4 %copy-start.8 = (f32[64]{0:T(128)S(1)}, f32[64]{0:T(128)}, u32[]{:S(2)}) copy-start(f32[64]{0:T(128)} %copy-done.7) | copy-start | bytes 772
  114.6 59.6 %copy-start.4 = (bf16[64,2048]{1,0:T(8,128)(2,1)S(1)}, bf16[64,2048]{1,0:T(8,128)(2,1)}, u32[]{:S(2)}) copy-start(bf16[64,2048]{1,0:T(8,128)(2,1)} %copy-done.3) | copy-start | bytes 786436
  114.6 59.6 %copy-start.10 = (pred[64]{0:T(512)(128)(4,1)S(1)}, pred[64]{0:T(512)(128)(4,1)}, u32[]{:S(2)}) copy-start(pred[64]{0:T(512)(128)(4,1)} %copy-done.9) | copy-start | bytes 196
  177.8 31.1 %all-to-all-start.1 = ((f32[16,1,1]{2,1,0:T(1,128)}), f32[16,1,1]{2,1,0:T(1,128)S(1)}, u32[]{:S(2)}, u32[]{:S(2)}) async-start(f32[16,1,1]{2,1,0:T(1,128)} %broadcast_in_dim.70), calls=%async_computation.1 | async-start | bytes 16384 | tf_op jit(solution)/shard_map/all_to_all | solution.py:41
Sparse Core Ops, SparseCore 0:
  176.7 279.7 all-reduce.1
where the time goes:
time: 467 us; the launch traced here: 466 us
  waiting for transfers between devices  261 us (56%)
  blocking collectives  79.1 us (17%)
  matrix products  57.3 us (12%)
  starting transfers between devices  30 us (6%)
  between operations  16.1 us (3%)
  other arithmetic  12.5 us (3%)
  local copies, waits for them, and re-layouts  10 us (2%)
    psum x1, waiting for transfers between devices, per_device(): summed = lax.psum(full, DP_PROTO)  244 us
    all_gather x4, blocking collectives, stacked_from(): blocks = lax.all_gather(blocks, axes[k])  53.1 us
    all_to_all x2, starting transfers between devices, sent_to_all(): lax.all_to_all(jnp.broadcast_to(array[None], (peers, *array.shape)), axis...  29.8 us
    all_to_all x1, blocking collectives, summed_on_arrival(): lax.all_to_all(in_blocks(array, dim, peers), axis, 0, 0, tiled=True)  26 us
    dot_general x2, matrix products, gradient_step(): return acc + jnp.dot(grads, tile, preferred_element_type=jnp.float32)  20.2 us
    dot_general x4, matrix products, block_logits(): lax.dot_general(student, tile, dims, preferred_element_type=jnp.float32)  18.1 us
    all_to_all x2, waiting for transfers between devices, sent_to_all(): lax.all_to_all(jnp.broadcast_to(array[None], (peers, *array.shape)), axis...  17 us
    dot_general x2, matrix products, block_logits(): lax.dot_general(teacher, tile, dims, preferred_element_type=jnp.float32)  11.9 us
  transfers between devices with their start and end apart: 3, of which 3 were waited for; matrix products, arithmetic and copies ran while one was open for 1% of the time, Pallas kernels for 0%

commit v1 on v0

v1 whole, which is shorter than its diff:
```python
import math

import jax
import jax.numpy as jnp
from jax import lax
from jax.experimental import pallas as pl
from jax.experimental.pallas import tpu as pltpu
from jax.sharding import Mesh
from jax.sharding import PartitionSpec as P

PROTO = ("proto_0", "proto_1")
DP_PROTO = ("dp", "proto_0", "proto_1")

STUDENT_TEMP = 0.1
TEACHER_TEMP = 0.07
LOSS_SCALE = 524288.0
EPSILON = 1e-06

LOG2E = 1.4426950408889634
LN2 = 0.6931471805599453
S_FACTOR = LOG2E / STUDENT_TEMP
T_FACTOR = LOG2E / TEACHER_TEMP

F32 = jnp.float32
BF16 = jnp.bfloat16
MESH = pl.DeviceIdType.MESH

DP = 16
NX = 2
NZ = 8
PEERS = NX * NZ
TILE = 512
KTILE = 1024


def contract(left, right, dims):
    return lax.dot_general(left, right, (dims, ((), ())), preferred_element_type=F32)


def kernel(
    masks,
    hidden_hbm,
    teacher_hbm,
    weight_hbm,
    protos_hbm,
    center,
    loss_out,
    hidden_out,
    head_out,
    hidden,
    feats,
    weight,
    protos,
    protos_t,
    centers,
    rows_all,
    s_all,
    t_all,
    unit_ref,
    radius_ref,
    picked_mine,
    picked_all,
    stats,
    stats_all,
    top,
    grads,
    total,
    parts,
    parts_all,
    dirs,
    losses,
    losses_p,
    heads,
    heads_all,
    load_sem,
    row_send,
    row_recv,
    pick_send,
    pick_recv,
    stat_send,
    stat_recv,
    part_send,
    part_recv,
    dir_send,
    dir_recv,
    pass_send,
    loss_send,
    loss_recv,
    lossp_send,
    lossp_recv,
    head_send,
    head_recv,
):
    d = lax.axis_index("dp")
    a = lax.axis_index("proto_0")
    z = lax.axis_index("proto_1")
    b = 1 - a
    p = a * NZ + z
    images, patches, _ = hidden.shape
    picks = masks.shape[1]
    rows = images * picks
    bottleneck = weight.shape[1]
    table = protos.shape[0]
    tiles = table // TILE
    lines = TILE // 8
    pending = []

    def send(src, dst, send_sem, recv_sem, device):
        copy = pltpu.make_async_remote_copy(
            src_ref=src,
            dst_ref=dst,
            send_sem=send_sem,
            recv_sem=recv_sem,
            device_id=device,
            device_id_type=MESH,
        )
        copy.start()
        pending.append(copy)

    def arrived(ref, sem):
        pltpu.make_async_remote_copy(
            src_ref=ref,
            dst_ref=ref,
            send_sem=sem,
            recv_sem=sem,
            device_id={"proto_0": b},
            device_id_type=MESH,
        ).wait_recv()

    def proto_peer(k):
        peer = (p + k) % PEERS
        return peer, {"proto_0": peer // NZ, "proto_1": peer % NZ}

    def dp_peer(k):
        peer = (d + k) % DP
        return peer, {"dp": peer}

    loads = [
        pltpu.make_async_copy(src, dst, load_sem.at[k])
        for k, (src, dst) in enumerate(
            (
                (hidden_hbm, hidden),
                (weight_hbm, weight),
                (teacher_hbm, feats),
                (protos_hbm, protos),
            )
        )
    ]
    for load in loads:
        load.start()

    barrier = pltpu.get_barrier_semaphore()
    for k in range(1, PEERS):
        pl.semaphore_signal(barrier, inc=1, device_id=proto_peer(k)[1], device_id_type=MESH)
    for k in range(1, DP):
        pl.semaphore_signal(barrier, inc=1, device_id=dp_peer(k)[1], device_id_type=MESH)

    loads[0].wait()
    loads[1].wait()
    loads[2].wait()
    picked_parts = []
    teacher_parts = []
    for image in range(images):
        index = lax.broadcasted_iota(jnp.int32, (patches, picks), 0)
        hot = (index == masks[image : image + 1, :]).astype(F32).astype(BF16)
        picked_parts.append(contract(hot, hidden[image], ((0,), (0,))).astype(BF16))
        teacher_parts.append(contract(hot, feats[image], ((0,), (0,))))
    picked = jnp.concatenate(picked_parts, axis=0)
    chosen = jnp.concatenate(teacher_parts, axis=0)
    raw = contract(picked, weight[...], ((1,), (0,)))
    radius = jnp.sqrt(jnp.sum(raw * raw, axis=1, keepdims=True) + EPSILON)
    unit = raw / radius
    unit_ref[...] = unit
    radius_ref[...] = jnp.broadcast_to(radius, radius_ref.shape)
    length = jnp.sqrt(jnp.sum(chosen * chosen, axis=1, keepdims=True) + EPSILON)
    rows_all[z, a] = unit.astype(BF16)
    rows_all[z, 2 + a] = (chosen / length).astype(BF16)
    share = picked_mine.shape[2]
    for k in range(DP):
        picked_mine[k] = picked[:, k * share : (k + 1) * share]

    pl.semaphore_wait(barrier, PEERS + DP - 2)

    above = {"proto_1": (z + 1) % NZ}
    below = {"proto_1": (z + NZ - 1) % NZ}
    beside = {"proto_0": b}
    row_count = []

    def at(step):
        return (z + step) % NZ

    def slot(other, step, kind):
        return at(step % NZ), (b if other else a) + 2 * kind

    def row_pass(other, step, kind, device):
        line, column = slot(other, step, kind)
        ref = rows_all.at[line, column]
        send(ref, ref, row_send.at[len(row_count)], row_recv.at[line, column], device)
        row_count.append(0)

    def row_wait(other, step, kind):
        line, column = slot(other, step, kind)
        arrived(rows_all.at[line, column], row_recv.at[line, column])

    for kind in (0, 1):
        row_pass(0, 0, kind, above)
        row_pass(0, 0, kind, below)
        row_pass(0, 0, kind, beside)

    for k in range(1, DP):
        peer, device = dp_peer(k)
        send(picked_mine.at[peer], picked_all.at[d], pick_send.at[k], pick_recv.at[d], device)
    picked_all[d] = picked_mine[d]

    loads[3].wait()

    def turn(index, _):
        first = pl.multiple_of(index * 256, 256)
        protos_t[index] = protos[pl.ds(first, 256), :].T
        return 0

    lax.fori_loop(0, table // 256, turn, 0)

    def spread(index, _):
        line = center[pl.ds(index, 1), :]
        column = jnp.broadcast_to(line, (128, 128)).T
        centers[pl.ds(index * 16, 16)] = column.reshape(16, 8, 128)
        return 0

    lax.fori_loop(0, table // 128, spread, 0)

    def down(ref):
        return jnp.broadcast_to(ref, (8, 128))

    def logits_tile(index, line, state):
        peak_s, peak_t = state
        first = pl.multiple_of(index * TILE, TILE)
        tile = protos[pl.ds(first, TILE), :]
        both = contract(tile, rows_all[line].reshape(4 * rows, bottleneck), ((1,), (1,)))
        at_line = pl.ds(index * lines, lines)
        s = both[:, : 2 * rows].reshape(lines, 8, 128)
        t = both[:, 2 * rows :].reshape(lines, 8, 128) - centers[at_line]
        s_all[line, at_line] = s
        t_all[line, at_line] = t
        return jnp.maximum(peak_s, jnp.max(s, axis=0)), jnp.maximum(peak_t, jnp.max(t, axis=0))

    def weights_tile(index, line, peaks, state):
        total_s, total_t, cross = state
        at_line = pl.ds(index * lines, lines)
        s = s_all[line, at_line]
        power_s = jnp.exp2((s - peaks[0]) * S_FACTOR)
        power_t = jnp.exp2((t_all[line, at_line] - peaks[1]) * T_FACTOR)
        s_all[line, at_line] = power_s
        t_all[line, at_line] = power_t
        return (
            total_s + jnp.sum(power_s, axis=0),
            total_t + jnp.sum(power_t, axis=0),
            cross + jnp.sum(power_t * s, axis=0),
        )

    lowest = (jnp.full((8, 128), -jnp.inf, F32),) * 2
    zeros = (jnp.zeros((8, 128), F32),) * 3

    def peaks_of(state):
        return tuple(down(jnp.max(part, axis=0, keepdims=True)) for part in state)

    def finish(line, peaks, state):
        total_s, total_t, cross = (jnp.sum(part, axis=0, keepdims=True) for part in state)
        here = pl.ds(line, 1)
        shift_s = peaks[0][:1] * S_FACTOR
        shift_t = peaks[1][:1] * T_FACTOR
        top[0, here, :] = shift_s
        top[1, here, :] = shift_t
        top[2, here, :] = cross / total_t
        stats[0, here, :] = shift_s + jnp.log(total_s) * LOG2E
        stats[1, here, :] = shift_t + jnp.log(total_t) * LOG2E

    def first_pair(line):
        return peaks_of(
            lax.fori_loop(0, tiles, lambda i, state: logits_tile(i, line, state), lowest)
        )

    def pair(line, before, peaks):
        def body(index, state):
            return (
                logits_tile(index, line, state[0]),
                weights_tile(index, before, peaks, state[1]),
            )

        new, sums = lax.fori_loop(0, tiles, body, (lowest, zeros))
        finish(before, peaks, sums)
        return peaks_of(new)

    def last_pair(before, peaks):
        sums = lax.fori_loop(
            0, tiles, lambda i, state: weights_tile(i, before, peaks, state), zeros
        )
        finish(before, peaks, sums)

    for kind in (0, 1):
        row_wait(0, 1, kind)
        row_pass(0, 1, kind, below)
        row_pass(0, 1, kind, beside)
        row_wait(0, -1, kind)
        row_pass(0, -1, kind, above)
        row_pass(0, -1, kind, beside)
    row_wait(1, 0, 0)
    row_wait(1, 0, 1)
    peaks = first_pair(at(0))
    for kind in (0, 1):
        row_wait(0, 2, kind)
        row_pass(0, 2, kind, below)
        row_pass(0, 2, kind, beside)
        row_wait(0, -2, kind)
        row_pass(0, -2, kind, above)
        row_pass(0, -2, kind, beside)
    row_wait(1, 1, 0)
    row_wait(1, 1, 1)
    peaks = pair(at(1), at(0), peaks)
    row_wait(1, -1, 0)
    row_wait(1, -1, 1)
    peaks = pair(at(7), at(1), peaks)
    for kind in (0, 1):
        row_wait(1, 2, kind)
        row_pass(1, 2, kind, below)
        row_wait(1, -2, kind)
        row_pass(1, -2, kind, above)
    row_wait(0, 3, 0)
    row_pass(0, 3, 0, below)
    row_wait(0, -3, 1)
    row_pass(0, -3, 1, above)
    peaks = pair(at(2), at(7), peaks)
    row_wait(1, 3, 0)
    row_pass(1, 3, 0, below)
    row_wait(1, -3, 1)
    row_pass(1, -3, 1, above)
    peaks = pair(at(6), at(2), peaks)
    row_wait(0, 3, 1)
    row_wait(1, 3, 1)
    peaks = pair(at(3), at(6), peaks)
    row_wait(0, -3, 0)
    row_wait(1, -3, 0)
    peaks = pair(at(5), at(3), peaks)
    for kind in (0, 1):
        row_wait(0, 4, kind)
        row_wait(1, 4, kind)
    peaks = pair(at(4), at(5), peaks)
    last_pair(at(4), peaks)

    for k in range(1, PEERS):
        peer, device = proto_peer(k)
        send(stats, stats_all.at[p], stat_send.at[k], stat_recv.at[p], device)
    stats_all[p] = stats[...]
    for k in range(1, PEERS):
        peer = (p + k) % PEERS
        arrived(stats_all.at[peer], stat_recv.at[peer])
    every = stats_all[...]
    highest = jnp.max(every, axis=0)
    joined = highest + jnp.log(jnp.sum(jnp.exp2(every - highest), axis=0)) * LOG2E
    total_rows = rows * PEERS * DP
    factor = math.log2(LOSS_SCALE / (total_rows * STUDENT_TEMP))
    losses[d] = joined[0] * (LN2 / PEERS) - top[2] * jnp.exp2(stats[1] - joined[1]) / STUDENT_TEMP
    top[0] = jnp.exp2(top[0] - joined[0] + factor)
    top[1] = jnp.exp2(top[1] - joined[1] + factor)

    def part_of(line, chunk):
        here = pl.ds(chunk * (KTILE // 8), KTILE // 8)
        up = down(top[0, pl.ds(line, 1), :])
        off = down(top[1, pl.ds(line, 1), :])
        value = s_all[line, here] * up - t_all[line, here] * off
        return value.reshape(KTILE, 128).astype(BF16)

    def back_of(far, near):
        for chunk in range(table // KTILE):
            grads[chunk, :, :128] = part_of(far, chunk)
            grads[chunk, :, 128:] = part_of(near, chunk)
        for chunk in range(table // KTILE):
            left = jnp.concatenate(
                [protos_t[chunk * (KTILE // 256) + k] for k in range(KTILE // 256)], axis=1
            )
            product = contract(left, grads[chunk], ((1,), (0,)))
            if chunk == 0:
                total[...] = product
            else:
                total[...] += product
        turned = total[...].T
        parts[far] = turned[: 2 * rows].reshape(2, rows, bottleneck)
        parts[near] = turned[2 * rows :].reshape(2, rows, bottleneck)

    def give(line, column, k):
        send(
            parts.at[line, column],
            parts_all.at[p],
            part_send.at[k],
            part_recv.at[p],
            {"proto_0": column, "proto_1": line},
        )

    for step in range(NZ // 2):
        far, near = at(4 + step), at(3 - step)
        back_of(far, near)
        give(far, a, 4 * step)
        give(far, b, 4 * step + 1)
        if step < NZ // 2 - 1:
            give(near, a, 4 * step + 2)
        give(near, b, 4 * step + 3)

    back = parts[z, a]
    for k in range(1, PEERS):
        peer = (p + k) % PEERS
        arrived(parts_all.at[peer], part_recv.at[peer])
        back = back + parts_all[peer]

    unit = unit_ref[...]
    inner = jnp.sum(unit * back, axis=1, keepdims=True)
    direction = ((back - unit * inner) / radius_ref[:, :1]).astype(BF16)
    dirs[d] = direction

    pair_core = d + 1 - 2 * (d % 2)
    for k in range(1, DP // 2):
        send(
            dirs.at[d], dirs.at[d], dir_send.at[k], dir_recv.at[d], {"dp": (d + 2 * k) % DP}
        )
    send(dirs.at[d], dirs.at[d], dir_send.at[0], dir_recv.at[d], {"dp": pair_core})
    for k in range(1, DP):
        peer, device = dp_peer(k)
        send(losses.at[d], losses.at[d], loss_send.at[k], loss_recv.at[d], device)

    hidden_out[...] = contract(direction, weight[...], ((1,), (1,))).astype(BF16)

    for k in range(1, DP // 2):
        peer = (d + 2 * k) % DP
        arrived(dirs.at[peer], dir_recv.at[peer])
        send(
            dirs.at[peer], dirs.at[peer], pass_send.at[k], dir_recv.at[peer], {"dp": pair_core}
        )
    for k in range(1, DP):
        peer = (d + k) % DP
        arrived(losses.at[peer], loss_recv.at[peer])
        arrived(picked_all.at[peer], pick_recv.at[peer])
    losses_p[p] = jnp.sum(losses[...], axis=0)
    for k in range(1, PEERS):
        peer, device = proto_peer(k)
        send(losses_p.at[p], losses_p.at[p], lossp_send.at[k], lossp_recv.at[p], device)
    for k in range(DP // 2):
        peer = (pair_core + 2 * k) % DP
        arrived(dirs.at[peer], dir_recv.at[peer])

    share_rows = heads.shape[1]
    product = contract(
        picked_all[...].reshape(DP * rows, share),
        dirs[...].reshape(DP * rows, bottleneck),
        ((0,), (0,)),
    )
    heads[...] = product.reshape(PEERS, share_rows, bottleneck)
    for k in range(1, PEERS):
        peer, device = proto_peer(k)
        send(heads.at[peer], heads_all.at[p], head_send.at[k], head_recv.at[p], device)
    result = heads[p]
    loss = losses_p[p]
    for k in range(1, PEERS):
        peer = (p + k) % PEERS
        arrived(losses_p.at[peer], lossp_recv.at[peer])
        loss = loss + losses_p[peer]
        arrived(heads_all.at[peer], head_recv.at[peer])
        result = result + heads_all[peer]
    head_out[...] = result
    loss = jnp.sum(jnp.sum(loss, axis=0, keepdims=True), axis=1, keepdims=True)
    loss_out[...] = loss / total_rows

    for copy in pending:
        copy.wait_send()


def per_device(hidden_states, teacher_feats, masks, head_weight, prototypes, center):
    images, patches, width = hidden_states.shape
    bottleneck = head_weight.shape[1]
    table = prototypes.shape[0]
    rows = masks.shape[0] * masks.shape[1]
    share = width // DP
    dma = pltpu.SemaphoreType.DMA
    scratch = [
        pltpu.VMEM(hidden_states.shape, BF16),
        pltpu.VMEM(teacher_feats.shape, BF16),
        pltpu.VMEM(head_weight.shape, BF16),
        pltpu.VMEM(prototypes.shape, BF16),
        pltpu.VMEM((table // 256, bottleneck, 256), BF16),
        pltpu.VMEM((table // 8, 8, 128), F32),
        pltpu.VMEM((NZ, 4, rows, bottleneck), BF16),
        pltpu.VMEM((NZ, table // 8, 8, 128), F32),
        pltpu.VMEM((NZ, table // 8, 8, 128), F32),
        pltpu.VMEM((rows, bottleneck), F32),
        pltpu.VMEM((rows, 128), F32),
        pltpu.VMEM((DP, rows, share), BF16),
        pltpu.VMEM((DP, rows, share), BF16),
        pltpu.VMEM((2, 8, 128), F32),
        pltpu.VMEM((PEERS, 2, 8, 128), F32),
        pltpu.VMEM((3, 8, 128), F32),
        pltpu.VMEM((table // KTILE, KTILE, 256), BF16),
        pltpu.VMEM((bottleneck, 256), F32),
        pltpu.VMEM((NZ, 2, rows, bottleneck), F32),
        pltpu.VMEM((PEERS, rows, bottleneck), F32),
        pltpu.VMEM((DP, rows, bottleneck), BF16),
        pltpu.VMEM((DP, 8, 128), F32),
        pltpu.VMEM((PEERS, 8, 128), F32),
        pltpu.VMEM((PEERS, share // PEERS, bottleneck), F32),
        pltpu.VMEM((PEERS, share // PEERS, bottleneck), F32),
        dma((4,)),
        dma((32,)),
        dma((NZ, 4)),
        dma((DP,)),
        dma((DP,)),
        dma((PEERS,)),
        dma((PEERS,)),
        dma((PEERS,)),
        dma((PEERS,)),
        dma((DP // 2,)),
        dma((DP,)),
        dma((DP // 2,)),
        dma((DP,)),
        dma((DP,)),
        dma((PEERS,)),
        dma((PEERS,)),
        dma((PEERS,)),
        dma((PEERS,)),
    ]
    vmem = pl.BlockSpec(memory_space=pltpu.VMEM)
    anywhere = pl.BlockSpec(memory_space=pl.ANY)
    loss, grad_hidden, grad_head = pl.pallas_call(
        kernel,
        out_shape=(
            jax.ShapeDtypeStruct((1, 1), F32),
            jax.ShapeDtypeStruct((rows, width), BF16),
            jax.ShapeDtypeStruct((share // PEERS, bottleneck), F32),
        ),
        in_specs=[vmem, anywhere, anywhere, anywhere, anywhere, vmem],
        out_specs=(vmem, vmem, vmem),
        scratch_shapes=scratch,
        compiler_params=pltpu.CompilerParams(
            collective_id=0, has_side_effects=True, vmem_limit_bytes=60 * 1024 * 1024
        ),
        name="ibot",
    )(
        masks,
        hidden_states,
        teacher_feats,
        head_weight,
        prototypes,
        center.reshape(-1, 128),
    )
    return (loss.reshape(()), grad_hidden, grad_head)


def solution(mesh):
    finer = Mesh(mesh.devices.reshape(DP, NX, NZ), DP_PROTO)
    placed = (
        P(DP_PROTO, None, None),
        P(DP_PROTO, None, None),
        P(DP_PROTO, None),
        P(),
        P(PROTO, None),
        P(PROTO),
    )
    return jax.shard_map(
        per_device,
        mesh=finer,
        in_specs=placed,
        out_specs=(P(), P(DP_PROTO, None), P(DP_PROTO, None)),
        check_vma=False,
    )
```

time: 467 us -> 111 us (0.24)
  waiting for transfers between devices: 261 us -> 0 us
  Pallas kernels: 0 us -> 105 us
  blocking collectives: 79.1 us -> 0 us
  matrix products: 57.3 us -> 0 us
  starting transfers between devices: 30 us -> 0 us
  between operations: 16.1 us -> 2.31 us
  other arithmetic: 12.5 us -> 0 us
  local copies, waits for them, and re-layouts: 10 us -> 2.98 us
    psum x1 -> x0, waiting for transfers between devices: 244 us -> none  [per_device(): summed = lax.psum(full, DP_PROTO)]
    pallas_call x0 -> x1, Pallas kernels: none -> 105 us  [per_device(): pl.pallas_call(kernel, out_shape=(jax.ShapeDtypeStruct((1, 1), F32), jax....]
    dot_general x11 -> x0, matrix products: 57.3 us -> none  [the longest x2 20.2 us: gradient_step(): return acc + jnp.dot(grads, tile, preferred_element_type=jnp.float32)]
    all_gather x4 -> x0, blocking collectives: 53.1 us -> none  [stacked_from(): blocks = lax.all_gather(blocks, axes[k])]
    all_to_all x2 -> x0, starting transfers between devices: 29.8 us -> none  [sent_to_all(): lax.all_to_all(jnp.broadcast_to(array[None], (peers, *array.shape)), axis...]
    all_to_all x1 -> x0, blocking collectives: 26 us -> none  [summed_on_arrival(): lax.all_to_all(in_blocks(array, dim, peers), axis, 0, 0, tiled=True)]
    all_to_all x2 -> x0, waiting for transfers between devices: 17 us -> none  [sent_to_all(): lax.all_to_all(jnp.broadcast_to(array[None], (peers, *array.shape)), axis...]
    reduce_sum x7 -> x0, other arithmetic: 10.5 us -> none  [the longest x2 7.36 us: row_step(): cross = cross * rescale + jnp.sum(weights * s_logits, axis=1)]
  transfers between devices with their start and end apart: 3 -> 0, of which waited for: 3 -> 0; matrix products, arithmetic and copies ran while one was open for 1% -> 0% of each run, Pallas kernels for 0% -> 0%
where the time goes in v1:
time: 111 us; the launch traced here: 110 us
  Pallas kernels  105 us (95%)
  local copies, waits for them, and re-layouts  2.98 us (3%)
  between operations  2.31 us (2%)
    pallas_call x1, Pallas kernels, per_device(): pl.pallas_call(kernel, out_shape=(jax.ShapeDtypeStruct((1, 1), F32), jax....  105 us
    unnamed x2, local copies, waits for them, and re-layouts  2.98 us

profile of v1, /device:TPU:1, one launch (start us, length us, event | category | flops | bytes accessed | tf_op | source)
XLA Modules:
  0.0 110.5 jit_solution(8301232216932053983)
XLA Ops:
  0.6 105.2 %ibot.1 = (f32[1,1]{1,0:T(1,128)}, bf16[64,2048]{1,0:T(8,128)(2,1)}, f32[8,384]{1,0:T(8,128)}) custom-call(s32[2,32]{1,0:T(2,128)} %masks.1, bf16[2,256,2048]{2,1,0:T(8,128)(2,1)} %hidden_hbm.1, bf16[2,256,384]{2,1,0:T(8,128)(2,1)} %teacher_hbm.1, bf16[2048,384]{1,0:T(8,128)(2,1)} %weight_hbm.1, bf16[3072,384]{1,0:T(8,128)(2,1)} %protos_hbm.1, f32[24,128]{1,0:T(8,128)} %bitcast.2), custom_call_target="tpu_custom_call" | custom-call | tf_op jit(solution)/shard_map/ibot/pallas_call | solution.py:529
  106.4 1.7 %copy.13 = bf16[64,2048]{1,0:T(8,128)(2,1)} copy(bf16[64,2048]{1,0:T(8,128)(2,1)} %get-tuple-element.13) | data formatting | bytes 524288
  108.0 1.3 %copy.14 = f32[8,384]{1,0:T(8,128)} copy(f32[8,384]{1,0:T(8,128)} %get-tuple-element.14) | data formatting | bytes 24576

commit v2 on v1

--- a/solution.py
+++ b/solution.py
@@ -29,7 +29,7 @@
 NX = 2
 NZ = 8
 PEERS = NX * NZ
-TILE = 512
+TILE = 1536
 KTILE = 1024
 
 
@@ -54,8 +54,10 @@
     protos_t,
     centers,
     rows_all,
-    s_all,
-    t_all,
+    s_even,
+    s_odd,
+    t_even,
+    t_odd,
     unit_ref,
     radius_ref,
     picked_mine,
@@ -66,7 +68,9 @@
     grads,
     total,
     parts,
-    parts_all,
+    side_in,
+    up_in,
+    down_in,
     dirs,
     losses,
     losses_p,
@@ -79,8 +83,12 @@
     pick_recv,
     stat_send,
     stat_recv,
-    part_send,
-    part_recv,
+    side_send,
+    side_recv,
+    up_send,
+    up_recv,
+    down_send,
+    down_recv,
     dir_send,
     dir_recv,
     pass_send,
@@ -179,6 +187,13 @@
     for k in range(DP):
         picked_mine[k] = picked[:, k * share : (k + 1) * share]
 
+    loads[3].wait()
+    for index in range(table // 256):
+        protos_t[index] = protos[index * 256 : (index + 1) * 256, :].T
+    for index in range(table // 128):
+        column = jnp.broadcast_to(center[index : index + 1, :], (128, 128)).T
+        centers[index * 16 : (index + 1) * 16] = column.reshape(16, 8, 128)
+
     pl.semaphore_wait(barrier, PEERS + DP - 2)
 
     above = {"proto_1": (z + 1) % NZ}
@@ -212,46 +227,38 @@
         send(picked_mine.at[peer], picked_all.at[d], pick_send.at[k], pick_recv.at[d], device)
     picked_all[d] = picked_mine[d]
 
-    loads[3].wait()
-
-    def turn(index, _):
-        first = pl.multiple_of(index * 256, 256)
-        protos_t[index] = protos[pl.ds(first, 256), :].T
-        return 0
-
-    lax.fori_loop(0, table // 256, turn, 0)
-
-    def spread(index, _):
-        line = center[pl.ds(index, 1), :]
-        column = jnp.broadcast_to(line, (128, 128)).T
-        centers[pl.ds(index * 16, 16)] = column.reshape(16, 8, 128)
-        return 0
-
-    lax.fori_loop(0, table // 128, spread, 0)
-
     def down(ref):
         return jnp.broadcast_to(ref, (8, 128))
 
-    def logits_tile(index, line, state):
+    order = (0, 1, 7, 2, 6, 3, 5, 4)
+
+    def held(step):
+        place = order.index(step)
+        refs = (s_odd, t_odd) if place % 2 else (s_even, t_even)
+        return tuple(ref.at[place // 2] for ref in refs)
+
+    def logits_tile(index, step, state):
         peak_s, peak_t = state
+        s_ref, t_ref = held(step)
         first = pl.multiple_of(index * TILE, TILE)
         tile = protos[pl.ds(first, TILE), :]
-        both = contract(tile, rows_all[line].reshape(4 * rows, bottleneck), ((1,), (1,)))
+        both = contract(tile, rows_all[at(step)].reshape(4 * rows, bottleneck), ((1,), (1,)))
         at_line = pl.ds(index * lines, lines)
         s = both[:, : 2 * rows].reshape(lines, 8, 128)
         t = both[:, 2 * rows :].reshape(lines, 8, 128) - centers[at_line]
-        s_all[line, at_line] = s
-        t_all[line, at_line] = t
+        s_ref[at_line] = s
+        t_ref[at_line] = t
         return jnp.maximum(peak_s, jnp.max(s, axis=0)), jnp.maximum(peak_t, jnp.max(t, axis=0))
 
-    def weights_tile(index, line, peaks, state):
+    def weights_tile(index, step, peaks, state):
         total_s, total_t, cross = state
+        s_ref, t_ref = held(step)
         at_line = pl.ds(index * lines, lines)
-        s = s_all[line, at_line]
+        s = s_ref[at_line]
         power_s = jnp.exp2((s - peaks[0]) * S_FACTOR)
-        power_t = jnp.exp2((t_all[line, at_line] - peaks[1]) * T_FACTOR)
-        s_all[line, at_line] = power_s
-        t_all[line, at_line] = power_t
+        power_t = jnp.exp2((t_ref[at_line] - peaks[1]) * T_FACTOR)
+        s_ref[at_line] = power_s
+        t_ref[at_line] = power_t
         return (
             total_s + jnp.sum(power_s, axis=0),
             total_t + jnp.sum(power_t, axis=0),
@@ -264,9 +271,9 @@
     def peaks_of(state):
         return tuple(down(jnp.max(part, axis=0, keepdims=True)) for part in state)
 
-    def finish(line, peaks, state):
+    def finish(step, peaks, state):
         total_s, total_t, cross = (jnp.sum(part, axis=0, keepdims=True) for part in state)
-        here = pl.ds(line, 1)
+        here = pl.ds(at(step), 1)
         shift_s = peaks[0][:1] * S_FACTOR
         shift_t = peaks[1][:1] * T_FACTOR
         top[0, here, :] = shift_s
@@ -306,7 +313,7 @@
         row_pass(0, -1, kind, beside)
     row_wait(1, 0, 0)
     row_wait(1, 0, 1)
-    peaks = first_pair(at(0))
+    peaks = first_pair(0)
     for kind in (0, 1):
         row_wait(0, 2, kind)
         row_pass(0, 2, kind, below)
@@ -316,10 +323,10 @@
         row_pass(0, -2, kind, beside)
     row_wait(1, 1, 0)
     row_wait(1, 1, 1)
-    peaks = pair(at(1), at(0), peaks)
+    peaks = pair(1, 0, peaks)
     row_wait(1, -1, 0)
     row_wait(1, -1, 1)
-    peaks = pair(at(7), at(1), peaks)
+    peaks = pair(7, 1, peaks)
     for kind in (0, 1):
         row_wait(1, 2, kind)
         row_pass(1, 2, kind, below)
@@ -329,23 +336,23 @@
     row_pass(0, 3, 0, below)
     row_wait(0, -3, 1)
     row_pass(0, -3, 1, above)
-    peaks = pair(at(2), at(7), peaks)
+    peaks = pair(2, 7, peaks)
     row_wait(1, 3, 0)
     row_pass(1, 3, 0, below)
     row_wait(1, -3, 1)
     row_pass(1, -3, 1, above)
-    peaks = pair(at(6), at(2), peaks)
+    peaks = pair(6, 2, peaks)
     row_wait(0, 3, 1)
     row_wait(1, 3, 1)
-    peaks = pair(at(3), at(6), peaks)
+    peaks = pair(3, 6, peaks)
     row_wait(0, -3, 0)
     row_wait(1, -3, 0)
-    peaks = pair(at(5), at(3), peaks)
+    peaks = pair(5, 3, peaks)
     for kind in (0, 1):
         row_wait(0, 4, kind)
         row_wait(1, 4, kind)
-    peaks = pair(at(4), at(5), peaks)
-    last_pair(at(4), peaks)
+    peaks = pair(4, 5, peaks)
+    last_pair(4, peaks)
 
     for k in range(1, PEERS):
         peer, device = proto_peer(k)
@@ -363,11 +370,12 @@
     top[0] = jnp.exp2(top[0] - joined[0] + factor)
     top[1] = jnp.exp2(top[1] - joined[1] + factor)
 
-    def part_of(line, chunk):
+    def part_of(step, chunk):
+        s_ref, t_ref = held(step)
         here = pl.ds(chunk * (KTILE // 8), KTILE // 8)
-        up = down(top[0, pl.ds(line, 1), :])
-        off = down(top[1, pl.ds(line, 1), :])
-        value = s_all[line, here] * up - t_all[line, here] * off
+        up = down(top[0, pl.ds(at(step), 1), :])
+        off = down(top[1, pl.ds(at(step), 1), :])
+        value = s_ref[here] * up - t_ref[here] * off
         return value.reshape(KTILE, 128).astype(BF16)
 
     def back_of(far, near):
@@ -387,29 +395,54 @@
         parts[far] = turned[: 2 * rows].reshape(2, rows, bottleneck)
         parts[near] = turned[2 * rows :].reshape(2, rows, bottleneck)
 
-    def give(line, column, k):
+    half = rows // 2
+    for step in range(NZ // 2):
+        far, near = 4 + step, 3 - step
+        back_of(far, near)
+        for k in (far, near):
+            send(parts.at[k, b], side_in.at[k], side_send.at[k], side_recv.at[k], beside)
+
+    def gather_side(k):
+        arrived(side_in.at[k], side_recv.at[k])
+        parts[k, a] += side_in[k]
+
+    first_half, second_half = pl.ds(0, half), pl.ds(half, half)
+    gather_side(4)
+    send(
+        parts.at[4, a, first_half],
+        up_in.at[3, first_half],
+        up_send.at[3],
+        up_recv.at[3],
+        above,
+    )
+    send(
+        parts.at[4, a, second_half],
+        down_in.at[3, second_half],
+        down_send.at[3],
+        down_recv.at[3],
+        below,
+    )
+    for k in (3, 2, 1):
+        part = first_half if k == 3 else pl.ds(0, rows)
+        gather_side(k)
+        arrived(up_in.at[k, part], up_recv.at[k])
+        parts[k, a, part] += up_in[k, part]
+        send(parts.at[k, a], up_in.at[k - 1], up_send.at[k - 1], up_recv.at[k - 1], above)
+        part = second_half if k == 3 else pl.ds(0, rows)
+        gather_side(NZ - k)
+        arrived(down_in.at[k, part], down_recv.at[k])
+        parts[NZ - k, a, part] += down_in[k, part]
         send(
-            parts.at[line, column],
-            parts_all.at[p],
-            part_send.at[k],
-            part_recv.at[p],
-            {"proto_0": column, "proto_1": line},
-        )
-
-    for step in range(NZ // 2):
-        far, near = at(4 + step), at(3 - step)
-        back_of(far, near)
-        give(far, a, 4 * step)
-        give(far, b, 4 * step + 1)
-        if step < NZ // 2 - 1:
-            give(near, a, 4 * step + 2)
-        give(near, b, 4 * step + 3)
-
-    back = parts[z, a]
-    for k in range(1, PEERS):
-        peer = (p + k) % PEERS
-        arrived(parts_all.at[peer], part_recv.at[peer])
-        back = back + parts_all[peer]
+            parts.at[NZ - k, a],
+            down_in.at[k - 1],
+            down_send.at[k - 1],
+            down_recv.at[k - 1],
+            below,
+        )
+    arrived(side_in.at[0], side_recv.at[0])
+    arrived(up_in.at[0], up_recv.at[0])
+    arrived(down_in.at[0], down_recv.at[0])
+    back = (parts[0, a] + side_in[0]) + (up_in[0] + down_in[0])
 
     unit = unit_ref[...]
     inner = jnp.sum(unit * back, axis=1, keepdims=True)
@@ -487,8 +520,10 @@
         pltpu.VMEM((table // 256, bottleneck, 256), BF16),
         pltpu.VMEM((table // 8, 8, 128), F32),
         pltpu.VMEM((NZ, 4, rows, bottleneck), BF16),
-        pltpu.VMEM((NZ, table // 8, 8, 128), F32),
-        pltpu.VMEM((NZ, table // 8, 8, 128), F32),
+        pltpu.VMEM((NZ // 2, table // 8, 8, 128), F32),
+        pltpu.VMEM((NZ // 2, table // 8, 8, 128), F32),
+        pltpu.VMEM((NZ // 2, table // 8, 8, 128), F32),
+        pltpu.VMEM((NZ // 2, table // 8, 8, 128), F32),
         pltpu.VMEM((rows, bottleneck), F32),
         pltpu.VMEM((rows, 128), F32),
         pltpu.VMEM((DP, rows, share), BF16),
@@ -499,7 +534,9 @@
         pltpu.VMEM((table // KTILE, KTILE, 256), BF16),
         pltpu.VMEM((bottleneck, 256), F32),
         pltpu.VMEM((NZ, 2, rows, bottleneck), F32),
-        pltpu.VMEM((PEERS, rows, bottleneck), F32),
+        pltpu.VMEM((NZ, rows, bottleneck), F32),
+        pltpu.VMEM((4, rows, bottleneck), F32),
+        pltpu.VMEM((4, rows, bottleneck), F32),
         pltpu.VMEM((DP, rows, bottleneck), BF16),
         pltpu.VMEM((DP, 8, 128), F32),
         pltpu.VMEM((PEERS, 8, 128), F32),
@@ -512,8 +549,12 @@
         dma((DP,)),
         dma((PEERS,)),
         dma((PEERS,)),
-        dma((PEERS,)),
-        dma((PEERS,)),
+        dma((NZ,)),
+        dma((NZ,)),
+        dma((4,)),
+        dma((4,)),
+        dma((4,)),
+        dma((4,)),
         dma((DP // 2,)),
         dma((DP,)),
         dma((DP // 2,)),

time: 111 us -> 91.2 us (0.82)
  Pallas kernels: 105 us -> 85.6 us
    pallas_call x1, Pallas kernels: 105 us -> 85.6 us  [per_device(): pl.pallas_call(kernel, out_shape=(jax.ShapeDtypeStruct((1, 1), F32), jax....]
where the time goes in v2:
time: 91.2 us; the launch traced here: 90.9 us
  Pallas kernels  85.6 us (94%)
  local copies, waits for them, and re-layouts  2.98 us (3%)
  between operations  2.31 us (3%)
    pallas_call x1, Pallas kernels, per_device(): pl.pallas_call(kernel, out_shape=(jax.ShapeDtypeStruct((1, 1), F32), jax....  85.6 us
    unnamed x2, local copies, waits for them, and re-layouts  2.98 us

profile of v2, /device:TPU:1, one launch (start us, length us, event | category | flops | bytes accessed | tf_op | source)
XLA Modules:
  0.0 90.9 jit_solution(10935771582445041443)
XLA Ops:
  0.6 85.6 %ibot.1 = (f32[1,1]{1,0:T(1,128)}, bf16[64,2048]{1,0:T(8,128)(2,1)}, f32[8,384]{1,0:T(8,128)}) custom-call(s32[2,32]{1,0:T(2,128)} %masks.1, bf16[2,256,2048]{2,1,0:T(8,128)(2,1)} %hidden_hbm.1, bf16[2,256,384]{2,1,0:T(8,128)(2,1)} %teacher_hbm.1, bf16[2048,384]{1,0:T(8,128)(2,1)} %weight_hbm.1, bf16[3072,384]{1,0:T(8,128)(2,1)} %protos_hbm.1, f32[24,128]{1,0:T(8,128)} %bitcast.2), custom_call_target="tpu_custom_call" | custom-call | tf_op jit(solution)/shard_map/ibot/pallas_call | solution.py:570
  86.8 1.7 %copy.13 = bf16[64,2048]{1,0:T(8,128)(2,1)} copy(bf16[64,2048]{1,0:T(8,128)(2,1)} %get-tuple-element.13) | data formatting | bytes 524288
  88.4 1.3 %copy.14 = f32[8,384]{1,0:T(8,128)} copy(f32[8,384]{1,0:T(8,128)} %get-tuple-element.14) | data formatting | bytes 24576

commit v3 on v2

--- a/solution.py
+++ b/solution.py
@@ -38,15 +38,18 @@
 
 
 def kernel(
-    masks,
+    masks_hbm,
     hidden_hbm,
     teacher_hbm,
     weight_hbm,
     protos_hbm,
-    center,
+    center_hbm,
     loss_out,
     hidden_out,
     head_out,
+    masks,
+    center,
+    hidden_rows,
     hidden,
     feats,
     weight,
@@ -71,6 +74,8 @@
     side_in,
     up_in,
     down_in,
+    up_other,
+    down_other,
     dirs,
     losses,
     losses_p,
@@ -89,6 +94,10 @@
     up_recv,
     down_send,
     down_recv,
+    upo_send,
+    upo_recv,
+    downo_send,
+    downo_recv,
     dir_send,
     dir_recv,
     pass_send,
@@ -98,6 +107,7 @@
     lossp_recv,
     head_send,
     head_recv,
+    ready,
 ):
     d = lax.axis_index("dp")
     a = lax.axis_index("proto_0")
@@ -143,6 +153,15 @@
         peer = (d + k) % DP
         return peer, {"dp": peer}
 
+    barrier = pltpu.get_barrier_semaphore()
+    above = {"proto_1": (z + 1) % NZ}
+    below = {"proto_1": (z + NZ - 1) % NZ}
+    beside = {"proto_0": b}
+    partners = [{"dp": d + bit * (1 - 2 * ((d // bit) % 2))} for bit in (1, 2, 4, 8)]
+    greeted = [above, below, beside, *partners]
+    for device in greeted:
+        pl.semaphore_signal(barrier, inc=1, device_id=device, device_id_type=MESH)
+
     loads = [
         pltpu.make_async_copy(src, dst, load_sem.at[k])
         for k, (src, dst) in enumerate(
@@ -151,18 +170,15 @@
                 (weight_hbm, weight),
                 (teacher_hbm, feats),
                 (protos_hbm, protos),
+                (masks_hbm, masks),
+                (center_hbm, center),
             )
         )
     ]
-    for load in loads:
+    for load in (loads[4], *loads[:4], loads[5]):
         load.start()
 
-    barrier = pltpu.get_barrier_semaphore()
-    for k in range(1, PEERS):
-        pl.semaphore_signal(barrier, inc=1, device_id=proto_peer(k)[1], device_id_type=MESH)
-    for k in range(1, DP):
-        pl.semaphore_signal(barrier, inc=1, device_id=dp_peer(k)[1], device_id_type=MESH)
-
+    loads[4].wait()
     loads[0].wait()
     loads[1].wait()
     loads[2].wait()
@@ -188,45 +204,51 @@
         picked_mine[k] = picked[:, k * share : (k + 1) * share]
 
     loads[3].wait()
+    loads[5].wait()
     for index in range(table // 256):
         protos_t[index] = protos[index * 256 : (index + 1) * 256, :].T
     for index in range(table // 128):
         column = jnp.broadcast_to(center[index : index + 1, :], (128, 128)).T
         centers[index * 16 : (index + 1) * 16] = column.reshape(16, 8, 128)
 
-    pl.semaphore_wait(barrier, PEERS + DP - 2)
-
-    above = {"proto_1": (z + 1) % NZ}
-    below = {"proto_1": (z + NZ - 1) % NZ}
-    beside = {"proto_0": b}
+    pl.semaphore_wait(barrier, len(greeted))
+
+    above_two = {"proto_1": (z + 2) % NZ}
+    below_two = {"proto_1": (z + NZ - 2) % NZ}
     row_count = []
 
     def at(step):
         return (z + step) % NZ
 
-    def slot(other, step, kind):
-        return at(step % NZ), (b if other else a) + 2 * kind
-
-    def row_pass(other, step, kind, device):
-        line, column = slot(other, step, kind)
-        ref = rows_all.at[line, column]
-        send(ref, ref, row_send.at[len(row_count)], row_recv.at[line, column], device)
+    small = rows // 2
+
+    def slot(other, step, piece):
+        kind, side = divmod(piece, 2)
+        column = (b if other else a) + 2 * kind
+        here = pl.ds(side * small, small)
+        return rows_all.at[at(step % NZ), column, here], row_recv.at[at(step % NZ), column, side]
+
+    def row_pass(other, step, piece, device):
+        ref, sem = slot(other, step, piece)
+        send(ref, ref, row_send.at[len(row_count)], sem, device)
         row_count.append(0)
 
-    def row_wait(other, step, kind):
-        line, column = slot(other, step, kind)
-        arrived(rows_all.at[line, column], row_recv.at[line, column])
-
-    for kind in (0, 1):
-        row_pass(0, 0, kind, above)
-        row_pass(0, 0, kind, below)
-        row_pass(0, 0, kind, beside)
-
-    for k in range(1, DP):
-        peer, device = dp_peer(k)
-        send(picked_mine.at[peer], picked_all.at[d], pick_send.at[k], pick_recv.at[d], device)
-    picked_all[d] = picked_mine[d]
-
+    def row_wait(other, step, piece):
+        ref, sem = slot(other, step, piece)
+        arrived(ref, sem)
+
+    every_piece = range(4)
+    for piece in every_piece:
+        row_pass(0, 0, piece, beside)
+        row_pass(0, 0, piece, above)
+        row_pass(0, 0, piece, below)
+
+    def tell(turn):
+        pl.semaphore_signal(
+            ready.at[turn], inc=1, device_id=partners[turn], device_id_type=MESH
+        )
+
+    tell(0)
     def down(ref):
         return jnp.broadcast_to(ref, (8, 128))
 
@@ -304,53 +326,56 @@
         )
         finish(before, peaks, sums)
 
-    for kind in (0, 1):
-        row_wait(0, 1, kind)
-        row_pass(0, 1, kind, below)
-        row_pass(0, 1, kind, beside)
-        row_wait(0, -1, kind)
-        row_pass(0, -1, kind, above)
-        row_pass(0, -1, kind, beside)
-    row_wait(1, 0, 0)
-    row_wait(1, 0, 1)
+    for piece in every_piece:
+        for step, device in ((1, below), (-1, above)):
+            row_wait(0, step, piece)
+            row_pass(0, step, piece, device)
+            row_pass(0, step, piece, beside)
+    for piece in every_piece:
+        row_wait(1, 0, piece)
+    pl.semaphore_wait(ready.at[0], 1)
+    tell(1)
     peaks = first_pair(0)
-    for kind in (0, 1):
-        row_wait(0, 2, kind)
-        row_pass(0, 2, kind, below)
-        row_pass(0, 2, kind, beside)
-        row_wait(0, -2, kind)
-        row_pass(0, -2, kind, above)
-        row_pass(0, -2, kind, beside)
-    row_wait(1, 1, 0)
-    row_wait(1, 1, 1)
+    pl.semaphore_wait(ready.at[1], 1)
+    tell(2)
+    for piece in every_piece:
+        for step, device in ((2, below), (-2, above)):
+            row_wait(0, step, piece)
+            row_pass(0, step, piece, device)
+    for piece in every_piece:
+        for step, device in ((1, below), (-1, above)):
+            row_wait(1, step, piece)
+            row_pass(1, step, piece, device)
     peaks = pair(1, 0, peaks)
-    row_wait(1, -1, 0)
-    row_wait(1, -1, 1)
+    pl.semaphore_wait(ready.at[2], 1)
+    for piece in every_piece:
+        for step, device in ((3, below), (-3, above)):
+            row_wait(0, step, piece)
+            if (piece < 2) == (step > 0):
+                row_pass(0, step, piece, device)
+            row_pass(0, step, piece, beside)
     peaks = pair(7, 1, peaks)
-    for kind in (0, 1):
-        row_wait(1, 2, kind)
-        row_pass(1, 2, kind, below)
-        row_wait(1, -2, kind)
-        row_pass(1, -2, kind, above)
-    row_wait(0, 3, 0)
-    row_pass(0, 3, 0, below)
-    row_wait(0, -3, 1)
-    row_pass(0, -3, 1, above)
+    for piece in every_piece:
+        row_wait(1, 2, piece)
     peaks = pair(2, 7, peaks)
-    row_wait(1, 3, 0)
-    row_pass(1, 3, 0, below)
-    row_wait(1, -3, 1)
-    row_pass(1, -3, 1, above)
+    for piece in (0, 2, 1, 3):
+        row_wait(0, 4, piece)
+        row_pass(0, 4, piece, beside)
+    for k in range(1, DP):
+        peer, device = dp_peer(k)
+        send(picked_mine.at[peer], picked_all.at[d], pick_send.at[k], pick_recv.at[d], device)
+    picked_all[d] = picked_mine[d]
+    for piece in every_piece:
+        row_wait(1, -2, piece)
     peaks = pair(6, 2, peaks)
-    row_wait(0, 3, 1)
-    row_wait(1, 3, 1)
+    for piece in every_piece:
+        row_wait(1, 3, piece)
     peaks = pair(3, 6, peaks)
-    row_wait(0, -3, 0)
-    row_wait(1, -3, 0)
+    for piece in every_piece:
+        row_wait(1, -3, piece)
     peaks = pair(5, 3, peaks)
-    for kind in (0, 1):
-        row_wait(0, 4, kind)
-        row_wait(1, 4, kind)
+    for piece in every_piece:
+        row_wait(1, 4, piece)
     peaks = pair(4, 5, peaks)
     last_pair(4, peaks)
 
@@ -395,54 +420,101 @@
         parts[far] = turned[: 2 * rows].reshape(2, rows, bottleneck)
         parts[near] = turned[2 * rows :].reshape(2, rows, bottleneck)
 
-    half = rows // 2
+    quarter = rows // 4
+
+    def cut(piece):
+        return pl.ds(piece * quarter, quarter)
+
+    def give_side(step):
+        for piece in every_piece:
+            send(
+                parts.at[step, b, cut(piece)],
+                side_in.at[step, cut(piece)],
+                side_send.at[step, piece],
+                side_recv.at[step, piece],
+                beside,
+            )
+
+    def give_along(column, step, piece, target, sems, device):
+        send(
+            parts.at[step, column, cut(piece)],
+            target.at[cut(piece)],
+            sems[0].at[piece],
+            sems[1].at[piece],
+            device,
+        )
+
+    def take(column, step, piece, source, sem):
+        arrived(source.at[cut(piece)], sem.at[piece])
+        parts[step, column, cut(piece)] += source[cut(piece)]
+
+    def take_side(step, piece):
+        take(a, step, piece, side_in.at[step], side_recv.at[step])
+
+    def up(step, piece):
+        k = step - 1
+        device = above_two if step == 2 else above
+        give_along(a, step, piece, up_in.at[k], (up_send.at[k], up_recv.at[k]), device)
+
+    def low(step, piece):
+        k = (-step) % NZ - 1
+        device = below_two if step == 6 else below
+        give_along(a, step, piece, down_in.at[k], (down_send.at[k], down_recv.at[k]), device)
+
     for step in range(NZ // 2):
         far, near = 4 + step, 3 - step
         back_of(far, near)
         for k in (far, near):
-            send(parts.at[k, b], side_in.at[k], side_send.at[k], side_recv.at[k], beside)
-
-    def gather_side(k):
-        arrived(side_in.at[k], side_recv.at[k])
-        parts[k, a] += side_in[k]
-
-    first_half, second_half = pl.ds(0, half), pl.ds(half, half)
-    gather_side(4)
-    send(
-        parts.at[4, a, first_half],
-        up_in.at[3, first_half],
-        up_send.at[3],
-        up_recv.at[3],
-        above,
-    )
-    send(
-        parts.at[4, a, second_half],
-        down_in.at[3, second_half],
-        down_send.at[3],
-        down_recv.at[3],
-        below,
-    )
-    for k in (3, 2, 1):
-        part = first_half if k == 3 else pl.ds(0, rows)
-        gather_side(k)
-        arrived(up_in.at[k, part], up_recv.at[k])
-        parts[k, a, part] += up_in[k, part]
-        send(parts.at[k, a], up_in.at[k - 1], up_send.at[k - 1], up_recv.at[k - 1], above)
-        part = second_half if k == 3 else pl.ds(0, rows)
-        gather_side(NZ - k)
-        arrived(down_in.at[k, part], down_recv.at[k])
-        parts[NZ - k, a, part] += down_in[k, part]
-        send(
-            parts.at[NZ - k, a],
-            down_in.at[k - 1],
-            down_send.at[k - 1],
-            down_recv.at[k - 1],
-            below,
-        )
-    arrived(side_in.at[0], side_recv.at[0])
-    arrived(up_in.at[0], up_recv.at[0])
-    arrived(down_in.at[0], down_recv.at[0])
-    back = (parts[0, a] + side_in[0]) + (up_in[0] + down_in[0])
+            if k in (4, 3, 5, 0):
+                give_side(k)
+        if near == 2:
+            for piece in every_piece:
+                give_along(b, 2, piece, up_other, (upo_send, upo_recv), above)
+        if far == 6:
+            for piece in every_piece:
+                give_along(b, 6, piece, down_other, (downo_send, downo_recv), below)
+
+    for piece in (0, 1):
+        take_side(4, piece)
+        up(4, piece)
+    for piece in (2, 3):
+        take_side(4, piece)
+        low(4, piece)
+    for piece in (2, 3):
+        take_side(3, piece)
+        up(3, piece)
+        take_side(5, piece - 2)
+        low(5, piece - 2)
+    for piece in every_piece:
+        take(b, 1, piece, up_other, upo_recv)
+        take(b, 7, piece, down_other, downo_recv)
+    give_side(1)
+    give_side(7)
+    for piece in (0, 1):
+        take_side(3, piece)
+        take(a, 3, piece, up_in.at[3], up_recv.at[3])
+        up(3, piece)
+        take_side(5, piece + 2)
+        take(a, 5, piece + 2, down_in.at[3], down_recv.at[3])
+        low(5, piece + 2)
+    for piece in every_piece:
+        turned_piece = (piece + 2) % 4
+        take(a, 2, turned_piece, up_in.at[2], up_recv.at[2])
+        up(2, turned_piece)
+        take(a, 6, piece, down_in.at[2], down_recv.at[2])
+        low(6, piece)
+    for piece in every_piece:
+        take_side(1, piece)
+        up(1, piece)
+        take_side(7, piece)
+        low(7, piece)
+    for piece in every_piece:
+        take_side(0, piece)
+        take(a, 0, piece, up_in.at[0], up_recv.at[0])
+        take(a, 0, piece, down_in.at[0], down_recv.at[0])
+        take(a, 0, piece, up_in.at[1], up_recv.at[1])
+        take(a, 0, piece, down_in.at[1], down_recv.at[1])
+    back = parts[0, a]
 
     unit = unit_ref[...]
     inner = jnp.sum(unit * back, axis=1, keepdims=True)
@@ -450,22 +522,32 @@
     dirs[d] = direction
 
     pair_core = d + 1 - 2 * (d % 2)
-    for k in range(1, DP // 2):
+    def chip_peer(y_step, x_step):
+        return (d + 4 * y_step) % DP + 2 * x_step * (1 - 2 * ((d // 2) % 2))
+
+    chips = ((2, 1), (1, 1), (3, 1), (0, 1), (2, 0), (1, 0), (3, 0))
+    for k, steps in enumerate(chips):
         send(
-            dirs.at[d], dirs.at[d], dir_send.at[k], dir_recv.at[d], {"dp": (d + 2 * k) % DP}
+            dirs.at[d], dirs.at[d], dir_send.at[k + 1], dir_recv.at[d], {"dp": chip_peer(*steps)}
         )
     send(dirs.at[d], dirs.at[d], dir_send.at[0], dir_recv.at[d], {"dp": pair_core})
     for k in range(1, DP):
         peer, device = dp_peer(k)
         send(losses.at[d], losses.at[d], loss_send.at[k], loss_recv.at[d], device)
 
-    hidden_out[...] = contract(direction, weight[...], ((1,), (1,))).astype(BF16)
-
-    for k in range(1, DP // 2):
-        peer = (d + 2 * k) % DP
+    hidden_rows[...] = contract(direction, weight[...], ((1,), (1,))).astype(BF16)
+    store = pltpu.make_async_copy(hidden_rows, hidden_out, load_sem.at[0])
+    store.start()
+
+    for k, steps in enumerate(chips[5:] + chips[4:5] + chips[:4]):
+        peer = chip_peer(*steps)
         arrived(dirs.at[peer], dir_recv.at[peer])
         send(
-            dirs.at[peer], dirs.at[peer], pass_send.at[k], dir_recv.at[peer], {"dp": pair_core}
+            dirs.at[peer],
+            dirs.at[peer],
+            pass_send.at[k + 1],
+            dir_recv.at[peer],
+            {"dp": pair_core},
         )
     for k in range(1, DP):
         peer = (d + k) % DP
@@ -501,6 +583,7 @@
     loss = jnp.sum(jnp.sum(loss, axis=0, keepdims=True), axis=1, keepdims=True)
     loss_out[...] = loss / total_rows
 
+    store.wait()
     for copy in pending:
         copy.wait_send()
 
@@ -513,6 +596,9 @@
     share = width // DP
     dma = pltpu.SemaphoreType.DMA
     scratch = [
+        pltpu.VMEM(masks.shape, jnp.int32),
+        pltpu.VMEM((table // 128, 128), F32),
+        pltpu.VMEM((rows, width), BF16),
         pltpu.VMEM(hidden_states.shape, BF16),
         pltpu.VMEM(teacher_feats.shape, BF16),
         pltpu.VMEM(head_weight.shape, BF16),
@@ -537,20 +623,26 @@
         pltpu.VMEM((NZ, rows, bottleneck), F32),
         pltpu.VMEM((4, rows, bottleneck), F32),
         pltpu.VMEM((4, rows, bottleneck), F32),
+        pltpu.VMEM((rows, bottleneck), F32),
+        pltpu.VMEM((rows, bottleneck), F32),
         pltpu.VMEM((DP, rows, bottleneck), BF16),
         pltpu.VMEM((DP, 8, 128), F32),
         pltpu.VMEM((PEERS, 8, 128), F32),
         pltpu.VMEM((PEERS, share // PEERS, bottleneck), F32),
         pltpu.VMEM((PEERS, share // PEERS, bottleneck), F32),
-        dma((4,)),
-        dma((32,)),
-        dma((NZ, 4)),
+        dma((6,)),
+        dma((64,)),
+        dma((NZ, 4, 2)),
         dma((DP,)),
         dma((DP,)),
         dma((PEERS,)),
         dma((PEERS,)),
-        dma((NZ,)),
-        dma((NZ,)),
+        dma((NZ, 4)),
+        dma((NZ, 4)),
+        dma((4, 4)),
+        dma((4, 4)),
+        dma((4, 4)),
+        dma((4, 4)),
         dma((4,)),
         dma((4,)),
         dma((4,)),
@@ -564,6 +656,7 @@
         dma((PEERS,)),
         dma((PEERS,)),
         dma((PEERS,)),
+        pltpu.SemaphoreType.REGULAR((3,)),
     ]
     vmem = pl.BlockSpec(memory_space=pltpu.VMEM)
     anywhere = pl.BlockSpec(memory_space=pl.ANY)
@@ -574,8 +667,8 @@
             jax.ShapeDtypeStruct((rows, width), BF16),
             jax.ShapeDtypeStruct((share // PEERS, bottleneck), F32),
         ),
-        in_specs=[vmem, anywhere, anywhere, anywhere, anywhere, vmem],
-        out_specs=(vmem, vmem, vmem),
+        in_specs=[anywhere] * 6,
+        out_specs=(vmem, anywhere, vmem),
         scratch_shapes=scratch,
         compiler_params=pltpu.CompilerParams(
             collective_id=0, has_side_effects=True, vmem_limit_bytes=60 * 1024 * 1024
@@ -589,6 +682,17 @@
         prototypes,
         center.reshape(-1, 128),
     )
+    def hand(*refs):
+        for source, target in zip(refs[:3], refs[3:]):
+            target[...] = source[...]
+
+    loss, grad_hidden, grad_head = pl.pallas_call(
+        hand,
+        out_shape=tuple(
+            jax.ShapeDtypeStruct(part.shape, part.dtype) for part in (loss, grad_hidden, grad_head)
+        ),
+        name="hand",
+    )(loss, grad_hidden, grad_head)
     return (loss.reshape(()), grad_hidden, grad_head)
 
 

time: 91.2 us -> 83.2 us (0.912)
  Pallas kernels: 85.6 us -> 82.5 us
  local copies, waits for them, and re-layouts: 2.98 us -> 0 us
  between operations: 2.31 us -> 0.64 us
    pallas_call x1, Pallas kernels: 85.6 us -> 80.1 us  [per_device(): pl.pallas_call(kernel, out_shape=(jax.ShapeDtypeStruct((1, 1), F32), jax....]
    unnamed x2 -> x0, local copies, waits for them, and re-layouts: 2.98 us -> none
    pallas_call x0 -> x1, Pallas kernels: none -> 2.36 us  [per_device(): pl.pallas_call(hand, out_shape=tuple((jax.ShapeDtypeStruct(part.shape, pa...]
where the time goes in v3:
time: 83.2 us; the launch traced here: 83.1 us
  Pallas kernels  82.5 us (99%)
    pallas_call x1, Pallas kernels, per_device(): pl.pallas_call(kernel, out_shape=(jax.ShapeDtypeStruct((1, 1), F32), jax....  80.1 us
    pallas_call x1, Pallas kernels, per_device(): pl.pallas_call(hand, out_shape=tuple((jax.ShapeDtypeStruct(part.shape, pa...  2.36 us

profile of v3, /device:TPU:1, one launch (start us, length us, event | category | flops | bytes accessed | tf_op | source)
XLA Modules:
  0.0 83.1 jit_solution(137429902221980304)
XLA Ops:
  0.6 80.1 %ibot.1 = (f32[1,1]{1,0:T(1,128)}, bf16[64,2048]{1,0:T(8,128)(2,1)}, f32[8,384]{1,0:T(8,128)}) custom-call(s32[2,32]{1,0:T(2,128)} %masks_hbm.1, bf16[2,256,2048]{2,1,0:T(8,128)(2,1)} %hidden_hbm.1, bf16[2,256,384]{2,1,0:T(8,128)(2,1)} %teacher_hbm.1, bf16[2048,384]{1,0:T(8,128)(2,1)} %weight_hbm.1, bf16[3072,384]{1,0:T(8,128)(2,1)} %protos_hbm.1, ...), custom_call_target="tpu_custom_call" | custom-call | tf_op jit(solution)/shard_map/ibot/pallas_call | solution.py:663
  80.7 2.4 %hand.1 = (f32[1,1]{1,0:T(1,128)}, bf16[64,2048]{1,0:T(8,128)(2,1)}, f32[8,384]{1,0:T(8,128)}) custom-call(f32[1,1]{1,0:T(1,128)} %get-tuple-element.9.refs_0_, bf16[64,2048]{1,0:T(8,128)(2,1)} %get-tuple-element.10.refs_1_, f32[8,384]{1,0:T(8,128)} %get-tuple-element.11.refs_2_), custom_call_target="tpu_custom_call" | custom-call | tf_op jit(solution)/shard_map/hand/pallas_call | solution.py:689

commit v4 on v3

--- a/solution.py
+++ b/solution.py
@@ -30,7 +30,8 @@
 NZ = 8
 PEERS = NX * NZ
 TILE = 1536
-KTILE = 1024
+PART = 256
+KTILE = 256
 
 
 def contract(left, right, dims):
@@ -68,8 +69,6 @@
     stats,
     stats_all,
     top,
-    grads,
-    total,
     parts,
     side_in,
     up_in,
@@ -81,6 +80,7 @@
     losses_p,
     heads,
     heads_all,
+    heads_full,
     load_sem,
     row_send,
     row_recv,
@@ -120,7 +120,8 @@
     bottleneck = weight.shape[1]
     table = protos.shape[0]
     tiles = table // TILE
-    lines = TILE // 8
+    lines = PART // 8
+    cuts = TILE // PART
     pending = []
 
     def send(src, dst, send_sem, recv_sem, device):
@@ -262,8 +263,8 @@
     def logits_tile(index, step, state):
         peak_s, peak_t = state
         s_ref, t_ref = held(step)
-        first = pl.multiple_of(index * TILE, TILE)
-        tile = protos[pl.ds(first, TILE), :]
+        first = pl.multiple_of(index * PART, PART)
+        tile = protos[pl.ds(first, PART), :]
         both = contract(tile, rows_all[at(step)].reshape(4 * rows, bottleneck), ((1,), (1,)))
         at_line = pl.ds(index * lines, lines)
         s = both[:, : 2 * rows].reshape(lines, 8, 128)
@@ -304,17 +305,23 @@
         stats[0, here, :] = shift_s + jnp.log(total_s) * LOG2E
         stats[1, here, :] = shift_t + jnp.log(total_t) * LOG2E
 
+    def many(index, state, work, *given):
+        for k in range(cuts):
+            state = work(index * cuts + k, *given, state)
+        return state
+
     def first_pair(line):
         return peaks_of(
-            lax.fori_loop(0, tiles, lambda i, state: logits_tile(i, line, state), lowest)
+            lax.fori_loop(0, tiles, lambda i, state: many(i, state, logits_tile, line), lowest)
         )
 
     def pair(line, before, peaks):
         def body(index, state):
-            return (
-                logits_tile(index, line, state[0]),
-                weights_tile(index, before, peaks, state[1]),
-            )
+            new, sums = state
+            for k in range(cuts):
+                new = logits_tile(index * cuts + k, line, new)
+                sums = weights_tile(index * cuts + k, before, peaks, sums)
+            return new, sums
 
         new, sums = lax.fori_loop(0, tiles, body, (lowest, zeros))
         finish(before, peaks, sums)
@@ -322,7 +329,7 @@
 
     def last_pair(before, peaks):
         sums = lax.fori_loop(
-            0, tiles, lambda i, state: weights_tile(i, before, peaks, state), zeros
+            0, tiles, lambda i, state: many(i, state, weights_tile, before, peaks), zeros
         )
         finish(before, peaks, sums)
 
@@ -361,27 +368,27 @@
     for piece in (0, 2, 1, 3):
         row_wait(0, 4, piece)
         row_pass(0, 4, piece, beside)
+    for piece in every_piece:
+        row_wait(1, -2, piece)
+    peaks = pair(6, 2, peaks)
+    for piece in every_piece:
+        row_wait(1, 3, piece)
+    peaks = pair(3, 6, peaks)
+    for piece in every_piece:
+        row_wait(1, -3, piece)
+    peaks = pair(5, 3, peaks)
+    for piece in every_piece:
+        row_wait(1, 4, piece)
+    peaks = pair(4, 5, peaks)
+    last_pair(4, peaks)
+
+    for k in range(1, PEERS):
+        peer, device = proto_peer(k)
+        send(stats, stats_all.at[p], stat_send.at[k], stat_recv.at[p], device)
     for k in range(1, DP):
         peer, device = dp_peer(k)
         send(picked_mine.at[peer], picked_all.at[d], pick_send.at[k], pick_recv.at[d], device)
     picked_all[d] = picked_mine[d]
-    for piece in every_piece:
-        row_wait(1, -2, piece)
-    peaks = pair(6, 2, peaks)
-    for piece in every_piece:
-        row_wait(1, 3, piece)
-    peaks = pair(3, 6, peaks)
-    for piece in every_piece:
-        row_wait(1, -3, piece)
-    peaks = pair(5, 3, peaks)
-    for piece in every_piece:
-        row_wait(1, 4, piece)
-    peaks = pair(4, 5, peaks)
-    last_pair(4, peaks)
-
-    for k in range(1, PEERS):
-        peer, device = proto_peer(k)
-        send(stats, stats_all.at[p], stat_send.at[k], stat_recv.at[p], device)
     stats_all[p] = stats[...]
     for k in range(1, PEERS):
         peer = (p + k) % PEERS
@@ -404,19 +411,15 @@
         return value.reshape(KTILE, 128).astype(BF16)
 
     def back_of(far, near):
+        product = None
         for chunk in range(table // KTILE):
-            grads[chunk, :, :128] = part_of(far, chunk)
-            grads[chunk, :, 128:] = part_of(near, chunk)
-        for chunk in range(table // KTILE):
+            right = jnp.concatenate([part_of(far, chunk), part_of(near, chunk)], axis=1)
             left = jnp.concatenate(
                 [protos_t[chunk * (KTILE // 256) + k] for k in range(KTILE // 256)], axis=1
             )
-            product = contract(left, grads[chunk], ((1,), (0,)))
-            if chunk == 0:
-                total[...] = product
-            else:
-                total[...] += product
-        turned = total[...].T
+            piece = contract(left, right, ((1,), (0,)))
+            product = piece if product is None else product + piece
+        turned = product.T
         parts[far] = turned[: 2 * rows].reshape(2, rows, bottleneck)
         parts[near] = turned[2 * rows :].reshape(2, rows, bottleneck)
 
@@ -461,25 +464,24 @@
         device = below_two if step == 6 else below
         give_along(a, step, piece, down_in.at[k], (down_send.at[k], down_recv.at[k]), device)
 
-    for step in range(NZ // 2):
-        far, near = 4 + step, 3 - step
-        back_of(far, near)
-        for k in (far, near):
-            if k in (4, 3, 5, 0):
-                give_side(k)
-        if near == 2:
-            for piece in every_piece:
-                give_along(b, 2, piece, up_other, (upo_send, upo_recv), above)
-        if far == 6:
-            for piece in every_piece:
-                give_along(b, 6, piece, down_other, (downo_send, downo_recv), below)
-
+    back_of(4, 3)
+    give_side(4)
+    give_side(3)
+    back_of(5, 2)
+    give_side(5)
+    for piece in every_piece:
+        give_along(b, 2, piece, up_other, (upo_send, upo_recv), above)
+    back_of(6, 1)
+    for piece in every_piece:
+        give_along(b, 6, piece, down_other, (downo_send, downo_recv), below)
     for piece in (0, 1):
         take_side(4, piece)
         up(4, piece)
     for piece in (2, 3):
         take_side(4, piece)
         low(4, piece)
+    back_of(7, 0)
+    give_side(0)
     for piece in (2, 3):
         take_side(3, piece)
         up(3, piece)
@@ -567,18 +569,20 @@
         dirs[...].reshape(DP * rows, bottleneck),
         ((0,), (0,)),
     )
-    heads[...] = product.reshape(PEERS, share_rows, bottleneck)
+    product = product.reshape(PEERS, share_rows, bottleneck)
+    heads_full[...] = product
+    heads[...] = product.astype(BF16)
     for k in range(1, PEERS):
         peer, device = proto_peer(k)
         send(heads.at[peer], heads_all.at[p], head_send.at[k], head_recv.at[p], device)
-    result = heads[p]
+    result = heads_full[p]
     loss = losses_p[p]
     for k in range(1, PEERS):
         peer = (p + k) % PEERS
         arrived(losses_p.at[peer], lossp_recv.at[peer])
         loss = loss + losses_p[peer]
         arrived(heads_all.at[peer], head_recv.at[peer])
-        result = result + heads_all[peer]
+        result = result + heads_all[peer].astype(F32)
     head_out[...] = result
     loss = jnp.sum(jnp.sum(loss, axis=0, keepdims=True), axis=1, keepdims=True)
     loss_out[...] = loss / total_rows
@@ -617,8 +621,6 @@
         pltpu.VMEM((2, 8, 128), F32),
         pltpu.VMEM((PEERS, 2, 8, 128), F32),
         pltpu.VMEM((3, 8, 128), F32),
-        pltpu.VMEM((table // KTILE, KTILE, 256), BF16),
-        pltpu.VMEM((bottleneck, 256), F32),
         pltpu.VMEM((NZ, 2, rows, bottleneck), F32),
         pltpu.VMEM((NZ, rows, bottleneck), F32),
         pltpu.VMEM((4, rows, bottleneck), F32),
@@ -628,7 +630,8 @@
         pltpu.VMEM((DP, rows, bottleneck), BF16),
         pltpu.VMEM((DP, 8, 128), F32),
         pltpu.VMEM((PEERS, 8, 128), F32),
-        pltpu.VMEM((PEERS, share // PEERS, bottleneck), F32),
+        pltpu.VMEM((PEERS, share // PEERS, bottleneck), BF16),
+        pltpu.VMEM((PEERS, share // PEERS, bottleneck), BF16),
         pltpu.VMEM((PEERS, share // PEERS, bottleneck), F32),
         dma((6,)),
         dma((64,)),

time: 83.2 us -> 79.1 us (0.951)
  Pallas kernels: 82.5 us -> 78.4 us
    pallas_call x1, Pallas kernels: 80.1 us -> 76 us  [per_device(): pl.pallas_call(kernel, out_shape=(jax.ShapeDtypeStruct((1, 1), F32), jax....]
where the time goes in v4:
time: 79.1 us; the launch traced here: 79 us
  Pallas kernels  78.4 us (99%)
    pallas_call x1, Pallas kernels, per_device(): pl.pallas_call(kernel, out_shape=(jax.ShapeDtypeStruct((1, 1), F32), jax....  76 us
    pallas_call x1, Pallas kernels, per_device(): pl.pallas_call(hand, out_shape=tuple((jax.ShapeDtypeStruct(part.shape, pa...  2.36 us

profile of v4, /device:TPU:1, one launch (start us, length us, event | category | flops | bytes accessed | tf_op | source)
XLA Modules:
  0.0 79.0 jit_solution(14886351313562414395)
XLA Ops:
  0.6 76.0 %ibot.1 = (f32[1,1]{1,0:T(1,128)}, bf16[64,2048]{1,0:T(8,128)(2,1)}, f32[8,384]{1,0:T(8,128)}) custom-call(s32[2,32]{1,0:T(2,128)} %masks_hbm.1, bf16[2,256,2048]{2,1,0:T(8,128)(2,1)} %hidden_hbm.1, bf16[2,256,384]{2,1,0:T(8,128)(2,1)} %teacher_hbm.1, bf16[2048,384]{1,0:T(8,128)(2,1)} %weight_hbm.1, bf16[3072,384]{1,0:T(8,128)(2,1)} %protos_hbm.1, ...), custom_call_target="tpu_custom_call" | custom-call | tf_op jit(solution)/shard_map/ibot/pallas_call | solution.py:666
  76.7 2.4 %hand.1 = (f32[1,1]{1,0:T(1,128)}, bf16[64,2048]{1,0:T(8,128)(2,1)}, f32[8,384]{1,0:T(8,128)}) custom-call(f32[1,1]{1,0:T(1,128)} %get-tuple-element.9.refs_0_, bf16[64,2048]{1,0:T(8,128)(2,1)} %get-tuple-element.10.refs_1_, f32[8,384]{1,0:T(8,128)} %get-tuple-element.11.refs_2_), custom_call_target="tpu_custom_call" | custom-call | tf_op jit(solution)/shard_map/hand/pallas_call | solution.py:692

commit v5 on v4

--- a/solution.py
+++ b/solution.py
@@ -81,6 +81,7 @@
     heads,
     heads_all,
     heads_full,
+    turned_picks,
     load_sem,
     row_send,
     row_recv,
@@ -146,9 +147,15 @@
             device_id_type=MESH,
         ).wait_recv()
 
+    places = sorted(
+        ((x, line) for x in range(NX) for line in range(NZ) if x or line),
+        key=lambda place: -(place[0] + min(place[1], NZ - place[1])),
+    )
+
     def proto_peer(k):
-        peer = (p + k) % PEERS
-        return peer, {"proto_0": peer // NZ, "proto_1": peer % NZ}
+        x, line = places[k - 1]
+        column, line = (b if x else a), (z + line) % NZ
+        return column * NZ + line, {"proto_0": column, "proto_1": line}
 
     def dp_peer(k):
         peer = (d + k) % DP
@@ -204,6 +211,44 @@
     for k in range(DP):
         picked_mine[k] = picked[:, k * share : (k + 1) * share]
 
+    pl.semaphore_wait(barrier, len(greeted))
+
+    above_two = {"proto_1": (z + 2) % NZ}
+    below_two = {"proto_1": (z + NZ - 2) % NZ}
+    row_count = []
+
+    def at(step):
+        return (z + step) % NZ
+
+    small = rows // 2
+
+    def slot(other, step, piece):
+        kind, side = divmod(piece, 2)
+        column = (b if other else a) + 2 * kind
+        here = pl.ds(side * small, small)
+        return rows_all.at[at(step % NZ), column, here], row_recv.at[at(step % NZ), column, side]
+
+    def row_pass(other, step, piece, device):
+        ref, sem = slot(other, step, piece)
+        send(ref, ref, row_send.at[len(row_count)], sem, device)
+        row_count.append(0)
+
+    def row_wait(other, step, piece):
+        ref, sem = slot(other, step, piece)
+        arrived(ref, sem)
+
+    every_piece = range(4)
+    for piece in every_piece:
+        row_pass(0, 0, piece, beside)
+        row_pass(0, 0, piece, above)
+        row_pass(0, 0, piece, below)
+
+    def tell(turn):
+        pl.semaphore_signal(
+            ready.at[turn], inc=1, device_id=partners[turn], device_id_type=MESH
+        )
+
+    tell(0)
     loads[3].wait()
     loads[5].wait()
     for index in range(table // 256):
@@ -212,44 +257,6 @@
         column = jnp.broadcast_to(center[index : index + 1, :], (128, 128)).T
         centers[index * 16 : (index + 1) * 16] = column.reshape(16, 8, 128)
 
-    pl.semaphore_wait(barrier, len(greeted))
-
-    above_two = {"proto_1": (z + 2) % NZ}
-    below_two = {"proto_1": (z + NZ - 2) % NZ}
-    row_count = []
-
-    def at(step):
-        return (z + step) % NZ
-
-    small = rows // 2
-
-    def slot(other, step, piece):
-        kind, side = divmod(piece, 2)
-        column = (b if other else a) + 2 * kind
-        here = pl.ds(side * small, small)
-        return rows_all.at[at(step % NZ), column, here], row_recv.at[at(step % NZ), column, side]
-
-    def row_pass(other, step, piece, device):
-        ref, sem = slot(other, step, piece)
-        send(ref, ref, row_send.at[len(row_count)], sem, device)
-        row_count.append(0)
-
-    def row_wait(other, step, piece):
-        ref, sem = slot(other, step, piece)
-        arrived(ref, sem)
-
-    every_piece = range(4)
-    for piece in every_piece:
-        row_pass(0, 0, piece, beside)
-        row_pass(0, 0, piece, above)
-        row_pass(0, 0, piece, below)
-
-    def tell(turn):
-        pl.semaphore_signal(
-            ready.at[turn], inc=1, device_id=partners[turn], device_id_type=MESH
-        )
-
-    tell(0)
     def down(ref):
         return jnp.broadcast_to(ref, (8, 128))
 
@@ -559,15 +566,14 @@
     for k in range(1, PEERS):
         peer, device = proto_peer(k)
         send(losses_p.at[p], losses_p.at[p], lossp_send.at[k], lossp_recv.at[p], device)
+    turned_picks[...] = picked_all[...].reshape(DP * rows, share).T
     for k in range(DP // 2):
         peer = (pair_core + 2 * k) % DP
         arrived(dirs.at[peer], dir_recv.at[peer])
 
     share_rows = heads.shape[1]
     product = contract(
-        picked_all[...].reshape(DP * rows, share),
-        dirs[...].reshape(DP * rows, bottleneck),
-        ((0,), (0,)),
+        turned_picks[...], dirs[...].reshape(DP * rows, bottleneck), ((1,), (0,))
     )
     product = product.reshape(PEERS, share_rows, bottleneck)
     heads_full[...] = product
@@ -633,6 +639,7 @@
         pltpu.VMEM((PEERS, share // PEERS, bottleneck), BF16),
         pltpu.VMEM((PEERS, share // PEERS, bottleneck), BF16),
         pltpu.VMEM((PEERS, share // PEERS, bottleneck), F32),
+        pltpu.VMEM((share, DP * rows), BF16),
         dma((6,)),
         dma((64,)),
         dma((NZ, 4, 2)),

time: 79.1 us -> 76.7 us (0.970)
  Pallas kernels: 78.4 us -> 76 us
    pallas_call x1, Pallas kernels: 76 us -> 73.6 us  [per_device(): pl.pallas_call(kernel, out_shape=(jax.ShapeDtypeStruct((1, 1), F32), jax....]
where the time goes in v5:
time: 76.7 us; the launch traced here: 76.6 us
  Pallas kernels  76 us (99%)
    pallas_call x1, Pallas kernels, per_device(): pl.pallas_call(kernel, out_shape=(jax.ShapeDtypeStruct((1, 1), F32), jax....  73.6 us
    pallas_call x1, Pallas kernels, per_device(): pl.pallas_call(hand, out_shape=tuple((jax.ShapeDtypeStruct(part.shape, pa...  2.36 us

profile of v5, /device:TPU:1, one launch (start us, length us, event | category | flops | bytes accessed | tf_op | source)
XLA Modules:
  0.0 76.6 jit_solution(2539421285087305743)
XLA Ops:
  0.6 73.6 %ibot.1 = (f32[1,1]{1,0:T(1,128)}, bf16[64,2048]{1,0:T(8,128)(2,1)}, f32[8,384]{1,0:T(8,128)}) custom-call(s32[2,32]{1,0:T(2,128)} %masks_hbm.1, bf16[2,256,2048]{2,1,0:T(8,128)(2,1)} %hidden_hbm.1, bf16[2,256,384]{2,1,0:T(8,128)(2,1)} %teacher_hbm.1, bf16[2048,384]{1,0:T(8,128)(2,1)} %weight_hbm.1, bf16[3072,384]{1,0:T(8,128)(2,1)} %protos_hbm.1, ...), custom_call_target="tpu_custom_call" | custom-call | tf_op jit(solution)/shard_map/ibot/pallas_call | solution.py:673
  74.2 2.4 %hand.1 = (f32[1,1]{1,0:T(1,128)}, bf16[64,2048]{1,0:T(8,128)(2,1)}, f32[8,384]{1,0:T(8,128)}) custom-call(f32[1,1]{1,0:T(1,128)} %get-tuple-element.9.refs_0_, bf16[64,2048]{1,0:T(8,128)(2,1)} %get-tuple-element.10.refs_1_, f32[8,384]{1,0:T(8,128)} %get-tuple-element.11.refs_2_), custom_call_target="tpu_custom_call" | custom-call | tf_op jit(solution)/shard_map/hand/pallas_call | solution.py:699

commit v6 on v5

--- a/solution.py
+++ b/solution.py
@@ -183,7 +183,7 @@
             )
         )
     ]
-    for load in (loads[4], *loads[:4], loads[5]):
+    for load in (loads[4], loads[2], *loads[:2], loads[3], loads[5]):
         load.start()
 
     loads[4].wait()
@@ -238,7 +238,8 @@
         arrived(ref, sem)
 
     every_piece = range(4)
-    for piece in every_piece:
+    arrival = (2, 3, 0, 1)
+    for piece in arrival:
         row_pass(0, 0, piece, beside)
         row_pass(0, 0, piece, above)
         row_pass(0, 0, piece, below)
@@ -340,51 +341,51 @@
         )
         finish(before, peaks, sums)
 
-    for piece in every_piece:
+    for piece in arrival:
         for step, device in ((1, below), (-1, above)):
             row_wait(0, step, piece)
             row_pass(0, step, piece, device)
             row_pass(0, step, piece, beside)
-    for piece in every_piece:
+    for piece in arrival:
         row_wait(1, 0, piece)
     pl.semaphore_wait(ready.at[0], 1)
     tell(1)
     peaks = first_pair(0)
     pl.semaphore_wait(ready.at[1], 1)
     tell(2)
-    for piece in every_piece:
+    for piece in arrival:
         for step, device in ((2, below), (-2, above)):
             row_wait(0, step, piece)
             row_pass(0, step, piece, device)
-    for piece in every_piece:
+    for piece in arrival:
         for step, device in ((1, below), (-1, above)):
             row_wait(1, step, piece)
             row_pass(1, step, piece, device)
     peaks = pair(1, 0, peaks)
     pl.semaphore_wait(ready.at[2], 1)
-    for piece in every_piece:
+    for piece in arrival:
         for step, device in ((3, below), (-3, above)):
             row_wait(0, step, piece)
             if (piece < 2) == (step > 0):
                 row_pass(0, step, piece, device)
             row_pass(0, step, piece, beside)
     peaks = pair(7, 1, peaks)
-    for piece in every_piece:
+    for piece in arrival:
         row_wait(1, 2, piece)
     peaks = pair(2, 7, peaks)
     for piece in (0, 2, 1, 3):
         row_wait(0, 4, piece)
         row_pass(0, 4, piece, beside)
-    for piece in every_piece:
+    for piece in arrival:
         row_wait(1, -2, piece)
     peaks = pair(6, 2, peaks)
-    for piece in every_piece:
+    for piece in arrival:
         row_wait(1, 3, piece)
     peaks = pair(3, 6, peaks)
-    for piece in every_piece:
+    for piece in arrival:
         row_wait(1, -3, piece)
     peaks = pair(5, 3, peaks)
-    for piece in every_piece:
+    for piece in arrival:
         row_wait(1, 4, piece)
     peaks = pair(4, 5, peaks)
     last_pair(4, peaks)

time: 76.7 us -> 77.1 us (level)
  no operation moved by 1% of the time
where the time goes in v6:
time: 77.1 us; the launch traced here: 77 us
  Pallas kernels  76.3 us (99%)
    pallas_call x1, Pallas kernels, per_device(): pl.pallas_call(kernel, out_shape=(jax.ShapeDtypeStruct((1, 1), F32), jax....  74 us
    pallas_call x1, Pallas kernels, per_device(): pl.pallas_call(hand, out_shape=tuple((jax.ShapeDtypeStruct(part.shape, pa...  2.36 us

profile of v6, /device:TPU:1, one launch (start us, length us, event | category | flops | bytes accessed | tf_op | source)
XLA Modules:
  0.0 77.0 jit_solution(6640190833614022210)
XLA Ops:
  0.6 74.0 %ibot.1 = (f32[1,1]{1,0:T(1,128)}, bf16[64,2048]{1,0:T(8,128)(2,1)}, f32[8,384]{1,0:T(8,128)}) custom-call(s32[2,32]{1,0:T(2,128)} %masks_hbm.1, bf16[2,256,2048]{2,1,0:T(8,128)(2,1)} %hidden_hbm.1, bf16[2,256,384]{2,1,0:T(8,128)(2,1)} %teacher_hbm.1, bf16[2048,384]{1,0:T(8,128)(2,1)} %weight_hbm.1, bf16[3072,384]{1,0:T(8,128)(2,1)} %protos_hbm.1, ...), custom_call_target="tpu_custom_call" | custom-call | tf_op jit(solution)/shard_map/ibot/pallas_call | solution.py:674
  74.6 2.4 %hand.1 = (f32[1,1]{1,0:T(1,128)}, bf16[64,2048]{1,0:T(8,128)(2,1)}, f32[8,384]{1,0:T(8,128)}) custom-call(f32[1,1]{1,0:T(1,128)} %get-tuple-element.9.refs_0_, bf16[64,2048]{1,0:T(8,128)(2,1)} %get-tuple-element.10.refs_1_, f32[8,384]{1,0:T(8,128)} %get-tuple-element.11.refs_2_), custom_call_target="tpu_custom_call" | custom-call | tf_op jit(solution)/shard_map/hand/pallas_call | solution.py:700
